TPU v7x, 32 devices: a 4x4x1 block of a 4x4x8 slice. The times are simulated.
32 devices in a mesh: dp: 1 (over z), tp: 4 (over y), fsdp: 4 (over x), cp: 2 (over core).
Axes of the slice: x: 4, y: 4, z: 1, core: 2. Of those that a mesh axis runs over, the one named last changes fastest.
The devices are a block of a 4x4x8 slice.
Arguments:
- hidden: bfloat16 [4, 3072, 5120], P(('dp', 'fsdp'), 'cp')
- positions: int32 [4, 3072], P(('dp', 'fsdp'), 'cp')
- attn_gain: float32 [5120], replicated
- w_query: bfloat16 [5120, 32, 128], P(('fsdp', 'cp'), 'tp')
- w_key: bfloat16 [5120, 8, 128], P(('fsdp', 'cp'), 'tp')
- w_value: bfloat16 [5120, 8, 128], P(('fsdp', 'cp'), 'tp')
- w_out: bfloat16 [32, 128, 5120], P('tp', None, ('fsdp', 'cp'))
- mlp_gain: float32 [5120], replicated
- w_gate: bfloat16 [5120, 14336], P(('fsdp', 'cp'), 'tp')
- w_up: bfloat16 [5120, 14336], P(('fsdp', 'cp'), 'tp')
- w_down: bfloat16 [14336, 5120], P('tp', ('fsdp', 'cp'))
Outputs:
- output: bfloat16 [4, 3072, 5120], P(('dp', 'fsdp'), 'cp')
All inputs are finite; a program needn't handle non-finite values.
Results may differ from a plain program's by a relative error of at most 0.0134593.
Values are sent between devices in bfloat16 or wider.
A program may use at most 768 MiB of HBM per device.

v0:
```python
import jax
import jax.numpy as jnp
from jax import lax
from jax.sharding import PartitionSpec as P, NamedSharding

ROPE_THETA = 500000.0
NORM_EPS = 1e-5
QBLOCK = 128
GROUP_AXES = ('fsdp', 'cp')


def rms_norm(hidden_f32, gain):
    mean_sq = jnp.mean(hidden_f32 * hidden_f32, axis=-1, keepdims=True)
    return (hidden_f32 * lax.rsqrt(mean_sq + NORM_EPS) * gain).astype(jnp.bfloat16)


def rope_tables(positions, head_dim):
    inv_freq = ROPE_THETA ** (-jnp.arange(0, head_dim, 2, dtype=jnp.float32) / head_dim)
    angles = positions.astype(jnp.float32)[..., None] * inv_freq
    return jnp.cos(angles)[..., None, :], jnp.sin(angles)[..., None, :]


def apply_rope(projected, rope_cos, rope_sin):
    half_dim = projected.shape[-1] // 2
    first_half = projected[..., :half_dim]
    second_half = projected[..., half_dim:]
    return jnp.concatenate([first_half * rope_cos - second_half * rope_sin, second_half * rope_cos + first_half * rope_sin], axis=-1)


def attention(queries, keys, values, q_pos, k_pos):
    n_seqs, tokens, kv_heads, group_size, head_dim = queries.shape
    n_blocks = tokens // QBLOCK
    q_blocks = queries.reshape(n_seqs * n_blocks, QBLOCK, kv_heads, group_size, head_dim)
    pos_blocks = q_pos.reshape(n_seqs * n_blocks, QBLOCK)
    seq_ids = jnp.arange(n_seqs * n_blocks) // n_blocks
    score_scale = head_dim ** -0.5

    def one_block(block_args):
        q_blk, qpos_blk, seq_id = block_args
        k_seq = lax.dynamic_index_in_dim(keys, seq_id, 0, keepdims=False)
        v_seq = lax.dynamic_index_in_dim(values, seq_id, 0, keepdims=False)
        kpos_seq = lax.dynamic_index_in_dim(k_pos, seq_id, 0, keepdims=False)
        scores = jnp.einsum('qkgd,skd->kgqs', q_blk, k_seq, preferred_element_type=jnp.float32) * score_scale
        visible = qpos_blk[:, None] >= kpos_seq[None, :]
        scores = jnp.where(visible, scores, -jnp.inf)
        row_max = jnp.max(scores, axis=-1, keepdims=True)
        probs = jnp.exp(scores - row_max)
        row_sum = jnp.sum(probs, axis=-1)
        weighted = jnp.einsum('kgqs,skd->qkgd', probs.astype(jnp.bfloat16), v_seq, preferred_element_type=jnp.float32)
        return (weighted / jnp.transpose(row_sum, (2, 0, 1))[..., None]).astype(jnp.bfloat16)

    mixed = lax.map(one_block, (q_blocks, pos_blocks, seq_ids))
    return mixed.reshape(n_seqs, tokens, kv_heads * group_size, head_dim)


def solution(mesh):
    seq_spec = P(('dp', 'fsdp'), 'cp', None)
    pos_spec = P(('dp', 'fsdp'), 'cp')
    in_spec = P(GROUP_AXES, 'tp', None)
    out_spec = P('tp', None, GROUP_AXES)
    col_spec = P(GROUP_AXES, 'tp')
    row_spec = P('tp', GROUP_AXES)
    rep_spec = P(None)

    def layer_local(hidden, positions, attn_gain, w_query, w_key, w_value, w_out, mlp_gain, w_gate, w_up, w_down):
        n_seqs, tokens, d_model = hidden.shape
        kv_heads = w_key.shape[1]
        head_dim = w_key.shape[2]
        group_size = w_query.shape[1] // kv_heads
        hidden_f32 = hidden.astype(jnp.float32)
        normed = rms_norm(hidden_f32, attn_gain)
        rope_cos, rope_sin = rope_tables(positions, head_dim)
        full_query = lax.all_gather(w_query, GROUP_AXES, axis=0, tiled=True)
        full_key = lax.all_gather(w_key, GROUP_AXES, axis=0, tiled=True)
        full_value = lax.all_gather(w_value, GROUP_AXES, axis=0, tiled=True)
        queries = apply_rope(jnp.einsum('bsd,dhe->bshe', normed, full_query, preferred_element_type=jnp.float32), rope_cos, rope_sin).astype(jnp.bfloat16)
        keys = apply_rope(jnp.einsum('bsd,dhe->bshe', normed, full_key, preferred_element_type=jnp.float32), rope_cos, rope_sin).astype(jnp.bfloat16)
        values = jnp.einsum('bsd,dhe->bshe', normed, full_value, preferred_element_type=jnp.float32).astype(jnp.bfloat16)
        all_keys = lax.all_gather(keys, 'cp', axis=1, tiled=True)
        all_values = lax.all_gather(values, 'cp', axis=1, tiled=True)
        all_pos = lax.all_gather(positions, 'cp', axis=1, tiled=True)
        mixed = attention(queries.reshape(n_seqs, tokens, kv_heads, group_size, head_dim), all_keys, all_values, positions, all_pos)
        full_out = lax.all_gather(w_out, GROUP_AXES, axis=2, tiled=True)
        attn_part = jnp.einsum('bshe,hed->bsd', mixed, full_out, preferred_element_type=jnp.float32).astype(jnp.bfloat16)
        attn_out = lax.psum(attn_part, 'tp')
        mid_f32 = (hidden_f32 + attn_out.astype(jnp.float32)).astype(jnp.bfloat16).astype(jnp.float32)
        normed_mlp = rms_norm(mid_f32, mlp_gain)
        full_gate = lax.all_gather(w_gate, GROUP_AXES, axis=0, tiled=True)
        full_up = lax.all_gather(w_up, GROUP_AXES, axis=0, tiled=True)
        gate_proj = jnp.einsum('bsd,df->bsf', normed_mlp, full_gate, preferred_element_type=jnp.float32)
        up_proj = jnp.einsum('bsd,df->bsf', normed_mlp, full_up, preferred_element_type=jnp.float32)
        act_mlp = (jax.nn.silu(gate_proj) * up_proj).astype(jnp.bfloat16)
        full_down = lax.all_gather(w_down, GROUP_AXES, axis=1, tiled=True)
        down_part = jnp.einsum('bsf,fd->bsd', act_mlp, full_down, preferred_element_type=jnp.float32).astype(jnp.bfloat16)
        down_proj = lax.psum(down_part, 'tp')
        return (mid_f32 + down_proj.astype(jnp.float32)).astype(jnp.bfloat16)

    return jax.shard_map(layer_local, mesh=mesh, in_specs=(seq_spec, pos_spec, rep_spec, in_spec, in_spec, in_spec, out_spec, rep_spec, col_spec, col_spec, row_spec), out_specs=seq_spec, check_vma=False)
```

profile of v0, /device:TPU:97, one launch (start us, length us, event | category | flops | bytes accessed | tf_op | source)
XLA Modules:
  0.0 1498.5 jit_solution(15509319735976073717)
XLA Ops:
  11.2 6.9 fusion.40
  19.6 17.1 %all-gather.13.cloned.1.call-done = bf16[5120,2,128]{0,2,1:T(8,128)(2,1)} async-done(((bf16[640,2,128]{0,2,1:T(8,128)(2,1)}), bf16[5120,2,128]{0,2,1:T(8,128)(2,1)}) %all-gather.13.cloned.1.call-update) | async-done | bytes 2621456 | tf_op jit(solution)/shard_map/all_gather | solution.py:74
  36.7 9.1 fusion.53
  49.3 13.0 all-gather.17.cloned.1.call-done
  62.3 11.8 fusion.60
  79.1 53.9 %all-gather.11.cloned.1.call-done = bf16[5120,8,128]{0,2,1:T(8,128)(2,1)} async-done(((bf16[640,8,128]{0,2,1:T(8,128)(2,1)}), bf16[5120,8,128]{0,2,1:T(8,128)(2,1)}) %all-gather.11.cloned.1.call-update) | async-done | bytes 10485776 | tf_op jit(solution)/shard_map/all_gather | solution.py:73
  133.0 23.1 %fusion.55 = f32[1536,1024]{0,1:S(1)} fusion(bf16[5120,1024]{0,1:T(8,128)(2,1)} %bitcast.152, bf16[1,1536,5120]{2,1,0:T(8,128)(2,1)} %param.13, f32[5120]{0:T(1024)S(1)} %copy-done.6, f32[1536]{0:T(1024)S(1)} %add_rsqrt_fusion.1), kind=kOutput, calls=%fused_computation.48 | convolution fusion | flops 16137584640 | bytes 32532480
  169.4 7.5 copy.21
  176.8 152.3 %while.11 = (s32[]{:T(128)}, bf16[12,128,2,4,128]{4,1,0,3,2:T(8,128)(2,1)}, s32[12,128]{1,0:T(8,128)S(1)}, s32[1,3072]{1,0:T(1,128)S(1)}, bf16[12,128,2,4,128]{4...) while((s32[]{:T(128)}, ...), condition=%wide.region_4.5_spmd, body=%wide.region_1.4_spmd.sunk | while | flops 1645869056 | bytes 43027032 | solution.py:52
  183.9 5.9 fusion.91
  196.6 5.9 fusion.91
  209.2 5.9 fusion.91
  221.9 5.9 fusion.91
  234.5 6.0 fusion.91
  247.2 5.9 fusion.91
  259.8 5.9 fusion.91
  272.5 6.0 fusion.91
  285.1 6.0 fusion.91
  297.8 6.0 fusion.91
  310.5 6.0 fusion.91
  323.1 6.0 fusion.91
  329.1 21.5 %fusion.49 = bf16[1,1536,5120]{2,1,0:T(8,128)(2,1)} fusion(bf16[1536,8,128]{2,0,1:T(8,128)(2,1)} %bitcast.155, bf16[8,128,5120]{2,1,0:T(8,128)(2,1)} %all-gather.19.cloned.1.call-done), kind=kOutput, calls=%fused_computation.42 | convolution fusion | flops 16113991680 | bytes 29360128 | tf_op jit(solution)/shard_map/bshe,hed->bsd/dot_general | solution.py:84
  352.9 271.0 %all-reduce.3.cloned.1.call-done = bf16[1,1536,5120]{2,1,0:T(8,128)(2,1)} async-done(((bf16[1,1536,5120]{2,1,0:T(8,128)(2,1)}), bf16[1,1536,5120]{2,1,0:T(8,128)(2,1)}) %all-reduce.3.cloned.1.call-update) | async-done | bytes 15728656 | tf_op jit(solution)/shard_map/psum | solution.py:85
  624.0 18.9 %fusion.44 = (f32[1536]{0:T(1024)S(1)}, bf16[1,1536,5120]{2,1,0:T(8,128)(2,1)}) fusion(bf16[1,1536,5120]{2,1,0:T(8,128)(2,1)} %all-reduce.3.cloned.1.call-done, bf16[1,1536,5120]{2,1,0:T(8,128)(2,1)} %param.13), kind=kLoop, calls=%fused_computation.34 | loop fusion | flops 55048704 | bytes 47192064 | tf_op jit(solution)/shard_map/reduce_sum | solution.py:13
  642.8 152.5 %all-gather.21.cloned.1.call-done = bf16[5120,3584]{1,0:T(8,128)(2,1)} async-done(((bf16[640,3584]{1,0:T(8,128)(2,1)}), bf16[5120,3584]{1,0:T(8,128)(2,1)}) %all-gather.21.cloned.1.call-update) | async-done | bytes 36700176 | tf_op jit(solution)/shard_map/all_gather | solution.py:88
  795.4 67.7 %fusion.58 = f32[1536,3584]{1,0:T(8,128)} fusion(bf16[5120,3584]{1,0:T(8,128)(2,1)} %all-gather.21.cloned.1.call-done, bf16[1,1536,5120]{2,1,0:T(8,128)(2,1)} %get-tuple-element.90, f32[5120]{0:T(1024)S(1)} %copy-done.7, f32[1536]{0:T(1024)S(1)} %add_rsqrt_fusion), kind=kOutput, calls=%fused_computation.50 | convolution fusion | flops 56402903040 | bytes 74475520 | tf_op jit(solution)/shard_map/bsd,df->bsf/dot_general | solution.py:90
  863.1 102.2 %all-gather.23.cloned.1.call-done = bf16[5120,3584]{1,0:T(8,128)(2,1)} async-done(((bf16[640,3584]{1,0:T(8,128)(2,1)}), bf16[5120,3584]{1,0:T(8,128)(2,1)}) %all-gather.23.cloned.1.call-update) | async-done | bytes 36700176 | tf_op jit(solution)/shard_map/all_gather | solution.py:89
  965.3 72.2 %multiply_convert_fusion = bf16[1536,3584]{1,0:T(8,128)(2,1)} fusion(f32[1536,3584]{1,0:T(8,128)} %fusion.58, bf16[5120,3584]{1,0:T(8,128)(2,1)} %all-gather.23.cloned.1.call-done, bf16[1,1536,5120]{2,1,0:T(8,128)(2,1)} %get-tuple-element.90, f32[5120]{0:T(1024)S(1)} %copy-done.7, f32[1536]{0:T(1024)S(1)} %add_rsqrt_fusion), kind=kOutput, calls=%fused_computation.39 | convolution fusion | flops 56435933184 | bytes 85485568 | tf_op jit(solution)/shard_map/bsd,df->bsf/dot_general | solution.py:91
  1037.4 97.3 %all-gather.25.cloned.1.call-done = bf16[3584,5120]{1,0:T(8,128)(2,1)} async-done(((bf16[3584,640]{1,0:T(8,128)(2,1)}), bf16[3584,5120]{1,0:T(8,128)(2,1)}) %all-gather.25.cloned.1.call-update) | async-done | bytes 36700176 | tf_op jit(solution)/shard_map/all_gather | solution.py:93
  1134.7 66.4 %fusion.48 = bf16[1,1536,5120]{2,1,0:T(8,128)(2,1)} fusion(bf16[1536,3584]{1,0:T(8,128)(2,1)} %multiply_convert_fusion, bf16[3584,5120]{1,0:T(8,128)(2,1)} %all-gather.25.cloned.1.call-done), kind=kOutput, calls=%fused_computation.41 | convolution fusion | flops 56379310080 | bytes 63438848 | tf_op jit(solution)/shard_map/bsf,fd->bsd/dot_general | solution.py:94
  1201.1 272.3 %all-reduce.5.cloned.1.call-done = bf16[1,1536,5120]{2,1,0:T(8,128)(2,1)} async-done(((bf16[1,1536,5120]{2,1,0:T(8,128)(2,1)}), bf16[1,1536,5120]{2,1,0:T(8,128)(2,1)}) %all-reduce.5.cloned.1.call-update) | async-done | bytes 15728656 | tf_op jit(solution)/shard_map/psum | solution.py:95
  1473.4 18.1 %fusion.47 = bf16[1,1536,5120]{2,1,0:T(8,128)(2,1)} fusion(bf16[1,1536,5120]{2,1,0:T(8,128)(2,1)} %get-tuple-element.90, bf16[1,1536,5120]{2,1,0:T(8,128)(2,1)} %all-reduce.5.cloned.1.call-done), kind=kLoop, calls=%fused_computation.37 | loop fusion | flops 31457280 | bytes 47185920 | tf_op jit(solution)/shard_map/convert_element_type | solution.py:96
  (107 shorter events, 110.4 us)
Async XLA Ops:
  6.5 30.2 %copy-start.6 = (f32[5120]{0:T(1024)S(1)}, f32[5120]{0:T(1024)}, u32[]{:S(2)}) copy-start(f32[5120]{0:T(1024)} %param.15) | copy-start | bytes 61444
  6.5 30.2 %all-gather.13.cloned.1.call-start = ((), (), s32[]{:S(2)}) async-start(), calls=%async_computation.1 | async-start | bytes 2949120 | tf_op jit(solution)/shard_map/all_gather | solution.py:74
  8.5 53.8 %all-gather.17.cloned.1.call-start = ((), (), s32[]{:S(2)}) async-start(), calls=%async_computation.3 | async-start | bytes 2949120 | tf_op jit(solution)/shard_map/all_gather | solution.py:75
  10.4 66.6 %all-gather.15.cloned.1.call-start = ((), (), s32[]{:S(2)}) async-start(), calls=%async_computation.2 | async-start | bytes 2359296 | tf_op jit(solution)/shard_map/all_gather | solution.py:79
  19.6 26.2 %copy-start = (f32[1536,64]{0,1:T(8,128)}, f32[1536,64]{0,1:T(8,128)S(1)}, u32[]{:S(2)}) copy-start(f32[1536,64]{0,1:T(8,128)S(1)} %get-tuple-element.97) | copy-start | bytes 1179652
  19.6 26.2 %copy-start.2 = (f32[1536,64]{0,1:T(8,128)}, f32[1536,64]{0,1:T(8,128)S(1)}, u32[]{:S(2)}) copy-start(f32[1536,64]{0,1:T(8,128)S(1)} %get-tuple-element.98) | copy-start | bytes 1179652
  36.7 10.4 copy-start.4
  47.1 85.9 %all-gather.11.cloned.1.call-start = ((), (), s32[]{:S(2)}) async-start(), calls=%async_computation | async-start | bytes 11796480 | tf_op jit(solution)/shard_map/all_gather | solution.py:73
  49.2 25.7 %copy-start.5 = (s32[1,1536]{1,0:T(1,128)S(1)}, s32[1,1536]{1,0:T(1,128)}, u32[]{:S(2)}) copy-start(s32[1,1536]{1,0:T(1,128)} %param.14) | copy-start | bytes 18436
  49.2 127.6 %all-gather.27.cloned.1.call-start = ((), (), s32[]{:S(2)}) async-start(), calls=%async_computation.10 | async-start | bytes 2359296 | tf_op jit(solution)/shard_map/all_gather | solution.py:80
  74.2 254.9 %all-gather.19.cloned.1.call-start = ((), (), s32[]{:S(2)}) async-start(), calls=%async_computation.4 | async-start | bytes 11796480 | tf_op jit(solution)/shard_map/all_gather | solution.py:83
  74.8 549.2 %all-reduce.3.cloned.1.call-start = ((), (), s32[]{:S(2)}) async-start(), calls=%async_computation.5 | async-start | bytes 31457280 | tf_op jit(solution)/shard_map/psum | solution.py:85
  133.0 23.1 %copy-start.1 = (f32[1536,64]{0,1:T(8,128)S(1)}, f32[1536,64]{0,1:T(8,128)}, u32[]{:S(2)}) copy-start(f32[1536,64]{0,1:T(8,128)} %copy-done) | copy-start | bytes 1179652
  133.0 23.1 %copy-start.3 = (f32[1536,64]{0,1:T(8,128)S(1)}, f32[1536,64]{0,1:T(8,128)}, u32[]{:S(2)}) copy-start(f32[1536,64]{0,1:T(8,128)} %copy-done.2) | copy-start | bytes 1179652
  350.6 444.8 %all-gather.21.cloned.1.call-start = ((), (), s32[]{:S(2)}) async-start(), calls=%async_computation.6 | async-start | bytes 41287680 | tf_op jit(solution)/shard_map/all_gather | solution.py:88
  351.4 613.9 %all-gather.23.cloned.1.call-start = ((), (), s32[]{:S(2)}) async-start(), calls=%async_computation.7 | async-start | bytes 41287680 | tf_op jit(solution)/shard_map/all_gather | solution.py:89
  352.2 782.5 %all-gather.25.cloned.1.call-start = ((), (), s32[]{:S(2)}) async-start(), calls=%async_computation.8 | async-start | bytes 41287680 | tf_op jit(solution)/shard_map/all_gather | solution.py:93
  352.9 442.5 %copy-start.7 = (f32[5120]{0:T(1024)S(1)}, f32[5120]{0:T(1024)}, u32[]{:S(2)}) copy-start(f32[5120]{0:T(1024)} %param.20) | copy-start | bytes 61444
  352.9 1120.5 %all-reduce.5.cloned.1.call-start = ((), (), s32[]{:S(2)}) async-start(), calls=%async_computation.9 | async-start | bytes 31457280 | tf_op jit(solution)/shard_map/psum | solution.py:95
Sparse Core Ops, SparseCore 0:
  8.9 27.7 all-gather.12
  38.3 23.9 all-gather.16
  63.9 10.2 all-gather.14
  75.6 57.2 all-gather.10
  134.4 10.0 all-gather.26
  145.9 57.2 all-gather.18
  350.7 273.2 all-reduce.2
  625.6 169.7 all-gather.20
  797.0 168.2 all-gather.22
  966.7 167.9 all-gather.24
  1201.3 272.0 all-reduce.4
where the time goes:
time: 1510 us; the launch traced here: 1500 us
  waiting for transfers between devices  982 us (65%)
  matrix products  382 us (25%)
  other arithmetic  95.6 us (6%)
  local copies, waits for them, and re-layouts  21.4 us (1%)
    psum x1, waiting for transfers between devices, layer_local(): down_proj = lax.psum(down_part, 'tp')  272 us
    psum x1, waiting for transfers between devices, layer_local(): attn_out = lax.psum(attn_part, 'tp')  271 us
    all_gather x1, waiting for transfers between devices, layer_local(): full_gate = lax.all_gather(w_gate, GROUP_AXES, axis=0, tiled=True)  153 us
    all_gather x1, waiting for transfers between devices, layer_local(): full_up = lax.all_gather(w_up, GROUP_AXES, axis=0, tiled=True)  102 us
    all_gather x1, waiting for transfers between devices, layer_local(): full_down = lax.all_gather(w_down, GROUP_AXES, axis=1, tiled=True)  97.3 us
    dot_general x1, matrix products, layer_local(): jnp.einsum('bsd,df->bsf', normed_mlp, full_up, preferred_element_type=jnp...  72.2 us
    dot_general x12, matrix products, one_block(): jnp.einsum('kgqs,skd->qkgd', probs.astype(jnp.bfloat16), v_seq, preferred...  71.4 us
    dot_general x1, matrix products, layer_local(): jnp.einsum('bsd,df->bsf', normed_mlp, full_gate, preferred_element_type=j...  67.7 us
  transfers between devices with their start and end apart: 11, of which 8 were waited for; matrix products, arithmetic and copies ran while one was open for 26% of the time, Pallas kernels for 0%

commit v1 on v0

v1 whole, which is shorter than its diff:
```python
import functools

import jax
import jax.numpy as jnp
from jax import lax
from jax.experimental import pallas as pl
from jax.experimental.pallas import tpu as pltpu
from jax.sharding import PartitionSpec as P

ROPE_THETA = 500000.0
NORM_EPS = 1e-5
GROUP_AXES = ('fsdp', 'cp')
N_SUB = 4
F32 = jnp.float32
BF16 = jnp.bfloat16
MESH = pl.DeviceIdType.MESH
VMEM_BIG = 58 * 1024 * 1024
ANY = pl.BlockSpec(memory_space=pl.ANY)


def rms_norm(hidden_f32, gain):
    mean_sq = jnp.mean(hidden_f32 * hidden_f32, axis=-1, keepdims=True)
    return (hidden_f32 * lax.rsqrt(mean_sq + NORM_EPS) * gain).astype(BF16)


def rope_tables(positions, head_dim):
    inv_freq = ROPE_THETA ** (-jnp.arange(0, head_dim, 2, dtype=F32) / head_dim)
    angles = positions.astype(F32)[..., None] * inv_freq
    cos, sin = jnp.cos(angles), jnp.sin(angles)
    return jnp.concatenate([cos, cos], axis=-1), jnp.concatenate([-sin, sin], axis=-1)


def qkv_kernel(head_dim, rope_heads, a_ref, w_ref, cos_ref, sin_ref, o_ref):
    cols = w_ref.shape[1]
    step = 4 * head_dim
    cos, sin = cos_ref[...], sin_ref[...]
    for start in range(0, cols, step):
        proj = jnp.dot(a_ref[...], w_ref[:, start:start + step], preferred_element_type=F32)
        for k in range(step // head_dim):
            x = proj[:, k * head_dim:(k + 1) * head_dim]
            if start // head_dim + k < rope_heads:
                x = x * cos + pltpu.roll(x, head_dim // 2, 1) * sin
            o_ref[:, start + k * head_dim:start + (k + 1) * head_dim] = x.astype(BF16)


def project_qkv(a, w, cos, sin, rope_heads):
    tokens, d_model = a.shape
    cols, head_dim = w.shape[1], cos.shape[1]
    rows = min(256, tokens)
    return pl.pallas_call(
        functools.partial(qkv_kernel, head_dim, rope_heads),
        grid=(tokens // rows,),
        out_shape=jax.ShapeDtypeStruct((tokens, cols), BF16),
        in_specs=[
            pl.BlockSpec((rows, d_model), lambda i: (i, 0)),
            pl.BlockSpec((d_model, cols), lambda i: (0, 0), pipeline_mode=pl.Buffered(1)),
            pl.BlockSpec((rows, head_dim), lambda i: (i, 0)),
            pl.BlockSpec((rows, head_dim), lambda i: (i, 0)),
        ],
        out_specs=pl.BlockSpec((rows, cols), lambda i: (i, 0)),
        compiler_params=pltpu.CompilerParams(vmem_limit_bytes=VMEM_BIG),
        cost_estimate=pl.CostEstimate(flops=2 * tokens * d_model * cols, bytes_accessed=2 * (tokens * d_model + d_model * cols + tokens * cols), transcendentals=0),
        name="qkv",
    )(a, w, cos, sin)


def attn_kernel(group, head_dim, per_seg, table_ref, q_ref, k_ref, v_ref, o_ref, m_sc, l_sc, acc_sc):
    blk = q_ref.shape[0]
    seg_rows = per_seg * blk
    qi = pl.program_id(1)
    true_seg = table_ref[4 + qi // per_seg]
    n_full = true_seg * per_seg + lax.rem(qi, per_seg)
    scale = (head_dim ** -0.5) * 1.4426950408889634
    m_sc[...] = jnp.full(m_sc.shape, -1e30, F32)
    l_sc[...] = jnp.zeros(l_sc.shape, F32)
    acc_sc[...] = jnp.zeros(acc_sc.shape, F32)

    def step(j, masked):
        row = table_ref[j // per_seg] * seg_rows + lax.rem(j, per_seg) * blk
        rows = pl.ds(pl.multiple_of(row, blk), blk)
        k, v = k_ref[rows, :], v_ref[rows, :]
        for h in range(group):
            q = q_ref[:, h * head_dim:(h + 1) * head_dim]
            s = lax.dot_general(q, k, (((1,), (1,)), ((), ())), preferred_element_type=F32)
            if masked:
                keep = lax.broadcasted_iota(jnp.int32, s.shape, 0) >= lax.broadcasted_iota(jnp.int32, s.shape, 1)
                s = jnp.where(keep, s, -1e30)
            m_old = m_sc[h, :, 0:1]
            m_new = jnp.maximum(m_old, jnp.max(s, axis=1, keepdims=True))
            alpha = jnp.exp2((m_old - m_new) * scale)
            p = jnp.exp2((s - m_new) * scale)
            part = p[:, 0:128]
            for c in range(128, blk, 128):
                part = part + p[:, c:c + 128]
            l_sc[h] = l_sc[h] * alpha + part
            acc_sc[h] = acc_sc[h] * alpha + jnp.dot(p.astype(BF16), v, preferred_element_type=F32)
            m_sc[h] = jnp.broadcast_to(m_new, m_sc.shape[1:])

    def body(j, carry):
        step(j, False)
        return carry

    lax.fori_loop(0, n_full, body, 0)
    step(n_full, True)
    for h in range(group):
        total = jnp.sum(l_sc[h], axis=1, keepdims=True)
        o_ref[:, h * head_dim:(h + 1) * head_dim] = (acc_sc[h] / total).astype(BF16)


def attention(qkv, kv_all, table, heads, kv_heads, head_dim):
    tokens, keys = qkv.shape[0], kv_all.shape[0]
    seg_rows = tokens // 2
    blk = min(256, seg_rows)
    per_seg = seg_rows // blk
    group = heads // kv_heads
    return pl.pallas_call(
        functools.partial(attn_kernel, group, head_dim, per_seg),
        grid_spec=pltpu.PrefetchScalarGridSpec(
            num_scalar_prefetch=1,
            grid=(kv_heads, tokens // blk),
            in_specs=[
                pl.BlockSpec((blk, group * head_dim), lambda g, i, t: (i, g)),
                pl.BlockSpec((keys, head_dim), lambda g, i, t: (0, g)),
                pl.BlockSpec((keys, head_dim), lambda g, i, t: (0, kv_heads + g)),
            ],
            out_specs=pl.BlockSpec((blk, group * head_dim), lambda g, i, t: (i, g)),
            scratch_shapes=[pltpu.VMEM((group, blk, 128), F32), pltpu.VMEM((group, blk, 128), F32), pltpu.VMEM((group, blk, head_dim), F32)],
        ),
        out_shape=jax.ShapeDtypeStruct((tokens, heads * head_dim), BF16),
        compiler_params=pltpu.CompilerParams(vmem_limit_bytes=32 * 1024 * 1024),
        cost_estimate=pl.CostEstimate(flops=2 * tokens * keys * heads * head_dim * 2, bytes_accessed=2 * (2 * tokens * heads * head_dim + 4 * keys * head_dim), transcendentals=tokens * keys * heads),
        name="attn",
    )(table, qkv, kv_all, kv_all)


def sum_kernel(n_tp, col_off, with_norm, n_after, lhs_hbm, w_hbm, res_hbm, gain_ref, *refs):
    refs = refs[n_after:]
    if with_norm:
        own_hbm, out_hbm = refs[:2]
        refs = refs[2:]
    else:
        out_hbm = refs[0]
        refs = refs[1:]
    lhs, w, part, in1, in2, res, own, norm, w_sem, l_sem, r_sem, o_sem, s1, r1, s2, r2, s3, r3, s4, r4 = refs
    n_w, depth, n_cols = w.shape
    cols = n_w * n_cols
    half = cols // 2
    rows = part.shape[2]
    block = rows * N_SUB
    me = lax.axis_index("tp")
    right, left = lax.rem(me + 1, n_tp), lax.rem(me + n_tp - 1, n_tp)
    far = lax.rem(me + 2, n_tp)
    sides = (right, left)
    lo, hi = pl.ds(0, half), pl.ds(half, half)
    halves = (lo, hi)

    def w_copy(d):
        return pltpu.make_async_copy(w_hbm.at[d], w.at[d], w_sem.at[d])

    lhs_copies = [pltpu.make_async_copy(lhs_hbm.at[pl.ds(b * block, block), :], lhs.at[b], l_sem.at[b]) for b in range(n_tp)]
    for c in lhs_copies:
        c.start()
    for d in range(n_w):
        w_copy(d).start()
    my_rows = pl.ds(pl.multiple_of(me * block, block), block)
    if with_norm:
        res_copies = [pltpu.make_async_copy(res_hbm.at[my_rows, :], res, r_sem.at[0])]
    else:
        wide = res_hbm.shape[1] // n_w
        res_copies = [pltpu.make_async_copy(res_hbm.at[:, pl.ds(d * wide + col_off, n_cols)], res.at[:, pl.ds(d * n_cols, n_cols)], r_sem.at[d]) for d in range(n_w)]
    for c in res_copies:
        c.start()

    barrier = pltpu.get_barrier_semaphore()
    for dev in sides:
        pl.semaphore_signal(barrier, inc=1, device_id={"tp": dev}, device_id_type=MESH)
    pl.semaphore_wait(barrier, 2)

    def remote(src, dst, send, recv, dev):
        return pltpu.make_async_remote_copy(src_ref=src, dst_ref=dst, send_sem=send, recv_sem=recv, device_id={"tp": dev}, device_id_type=MESH)

    def rows_of(b, s):
        return pl.ds(pl.multiple_of(b * block + s * rows, rows), rows)

    def hop1(s, i):
        return remote(part.at[s, far, :, halves[i]], in1.at[s, i], s1.at[s, i], r1.at[s, i], sides[i])

    def hop2(s, i):
        return remote(part.at[s, sides[i]], in2.at[s, i], s2.at[s, i], r2.at[s, i], sides[i])

    def hop3(s, i):
        return remote(norm.at[s], out_hbm.at[rows_of(me, s), :], s3.at[s, i], r3.at[s, i], sides[i])

    def hop4(s, i):
        block_rows = rows_of(sides[1 - i], s)
        where = out_hbm.at[block_rows, halves[i]]
        return remote(where, where, s4.at[s, i], r4.at[s, i], sides[i])

    def stage_a(s):
        left_rows = lhs[:, s * rows:(s + 1) * rows, :].reshape(n_tp * rows, depth)

        def one(d, carry):
            if s == 0:
                w_copy(d).wait()
            prod = jnp.dot(left_rows, w[d], preferred_element_type=F32).astype(BF16)
            part[s, :, :, pl.ds(pl.multiple_of(d * n_cols, n_cols), n_cols)] = prod.reshape(n_tp, rows, n_cols)
            return carry

        lax.fori_loop(0, n_w, one, 0)
        for i in range(2):
            hop1(s, i).start()

    def stage_b(s):
        for i in range(2):
            hop1(s, i).wait_recv()
            dest = sides[i]
            mine = part[s, dest, :, halves[i]].astype(F32)
            part[s, dest, :, halves[i]] = (mine + in1[s, i].astype(F32)).astype(BF16)
            hop2(s, i).start()

    def stage_c(s):
        for i in range(2):
            hop2(s, i).wait_recv()
        step = 16

        def one(k, carry):
            at = pl.ds(pl.multiple_of(k * step, step), step)
            total = part[s, me, at, :].astype(F32) + in2[s, 0, at, :].astype(F32) + in2[s, 1, at, :].astype(F32)
            total = total.astype(BF16).astype(F32)
            res_at = pl.ds(pl.multiple_of(s * rows + k * step, step), step)
            mid = (res[res_at, :].astype(F32) + total).astype(BF16)
            if with_norm:
                own[s, at, :] = mid
                mid = mid.astype(F32)
                mean_sq = jnp.mean(mid * mid, axis=-1, keepdims=True)
                mid = (mid * lax.rsqrt(mean_sq + NORM_EPS) * gain_ref[...]).astype(BF16)
            norm[s, at, :] = mid
            return carry

        lax.fori_loop(0, rows // step, one, 0)
        for i in range(2):
            hop3(s, i).start()
        local(s).start()
        if with_norm:
            keep(s).start()

    def local(s):
        return pltpu.make_async_copy(norm.at[s], out_hbm.at[rows_of(me, s), :], o_sem.at[s, 0])

    def keep(s):
        return pltpu.make_async_copy(own.at[s], own_hbm.at[pl.ds(s * rows, rows), :], o_sem.at[s, 1])

    def arrive3(s, i):
        where = out_hbm.at[rows_of(sides[1 - i], s), :]
        return remote(norm.at[s], where, s3.at[s, i], r3.at[s, i], sides[i])

    def arrive4(s, i):
        where = out_hbm.at[rows_of(far, s), halves[i]]
        return remote(where, where, s4.at[s, i], r4.at[s, i], sides[i])

    def stage_d(s):
        for i in range(2):
            arrive3(s, i).wait_recv()
            hop4(s, i).start()

    for c in lhs_copies:
        c.wait()
    for t in range(N_SUB + 3):
        if t < N_SUB:
            stage_a(t)
        if 0 <= t - 1 < N_SUB:
            stage_b(t - 1)
        if t == 1:
            for c in res_copies:
                c.wait()
        if 0 <= t - 2 < N_SUB:
            stage_c(t - 2)
        if 0 <= t - 3 < N_SUB:
            stage_d(t - 3)
    for s in range(N_SUB):
        local(s).wait()
        if with_norm:
            keep(s).wait()
        for i in range(2):
            hop1(s, i).wait_send()
            hop2(s, i).wait_send()
            hop3(s, i).wait_send()
            hop4(s, i).wait_send()
            arrive4(s, i).wait_recv()


def sum_over_tp(n_tp, lhs, w, res, gain, col_off, with_norm, collective_id, after=()):
    tokens, depth = lhs.shape
    n_w, _, n_cols = w.shape
    cols = n_w * n_cols
    block = tokens // n_tp
    rows = block // N_SUB
    out_shape = [jax.ShapeDtypeStruct((tokens, cols), BF16)]
    if with_norm:
        out_shape = [jax.ShapeDtypeStruct((block, cols), BF16)] + out_shape
    dma = pltpu.SemaphoreType.DMA
    small = (N_SUB, rows, cols) if with_norm else (1, 16, 128)
    scratch = [
        pltpu.VMEM((n_tp, block, depth), BF16),
        pltpu.VMEM((n_w, depth, n_cols), BF16),
        pltpu.VMEM((N_SUB, n_tp, rows, cols), BF16),
        pltpu.VMEM((N_SUB, 2, rows, cols // 2), BF16),
        pltpu.VMEM((N_SUB, 2, rows, cols), BF16),
        pltpu.VMEM((block, cols), BF16),
        pltpu.VMEM(small, BF16),
        pltpu.VMEM((N_SUB, rows, cols), BF16),
        dma((n_w,)), dma((n_tp,)), dma((n_w,)), dma((N_SUB, 2)),
    ] + [dma((N_SUB, 2))] * 8
    return pl.pallas_call(
        functools.partial(sum_kernel, n_tp, col_off, with_norm, len(after)),
        out_shape=out_shape,
        in_specs=[ANY, ANY, ANY, pl.BlockSpec(memory_space=pltpu.VMEM)] + [ANY] * len(after),
        out_specs=[ANY] * len(out_shape),
        scratch_shapes=scratch,
        compiler_params=pltpu.CompilerParams(collective_id=collective_id, has_side_effects=True, vmem_limit_bytes=VMEM_BIG),
        cost_estimate=pl.CostEstimate(flops=2 * tokens * cols * 30000, bytes_accessed=2 * (tokens * depth + depth * cols + 2 * tokens * cols), transcendentals=0),
        name="sum_tp_%d" % collective_id,
    )(lhs, w, res, gain, *after)


def join_kernel(n_w, a_ref, b_ref, o_ref):
    wa, wb = a_ref.shape[1] // n_w, b_ref.shape[1] // n_w
    for d in range(n_w):
        base = d * (wa + wb)
        o_ref[:, base:base + wa] = a_ref[:, d * wa:(d + 1) * wa]
        o_ref[:, base + wa:base + wa + wb] = b_ref[:, d * wb:(d + 1) * wb]


def join_columns(a, b, n_w):
    tokens = a.shape[0]
    rows = min(256, tokens)
    cols = a.shape[1] + b.shape[1]
    return pl.pallas_call(
        functools.partial(join_kernel, n_w),
        grid=(tokens // rows,),
        out_shape=jax.ShapeDtypeStruct((tokens, cols), BF16),
        in_specs=[pl.BlockSpec((rows, a.shape[1]), lambda i: (i, 0)), pl.BlockSpec((rows, b.shape[1]), lambda i: (i, 0))],
        out_specs=pl.BlockSpec((rows, cols), lambda i: (i, 0)),
        cost_estimate=pl.CostEstimate(flops=tokens * cols, bytes_accessed=4 * tokens * cols, transcendentals=0),
        name="join",
    )(a, b)


def solution(mesh):
    seq_spec = P(('dp', 'fsdp'), 'cp', None)
    pos_spec = P(('dp', 'fsdp'), 'cp')
    in_spec = P(GROUP_AXES, 'tp', None)
    out_spec = P('tp', None, GROUP_AXES)
    col_spec = P(GROUP_AXES, 'tp')
    row_spec = P('tp', GROUP_AXES)
    rep_spec = P(None)
    n_tp = mesh.shape['tp']
    n_w = mesh.shape['fsdp'] * mesh.shape['cp']

    def layer_local(hidden, positions, attn_gain, w_query, w_key, w_value, w_out, mlp_gain, w_gate, w_up, w_down):
        tokens, d_model = hidden.shape[1:]
        share, heads, head_dim = w_query.shape
        kv_heads = w_key.shape[1]
        w_qkv = jnp.concatenate([w.reshape(share, -1) for w in (w_query, w_key, w_value)], axis=1)
        full_qkv = lax.all_gather(w_qkv, GROUP_AXES, axis=0, tiled=True)
        full_out = lax.all_gather(w_out.reshape(heads * head_dim, share), GROUP_AXES, axis=0, tiled=False)
        full_gate = lax.all_gather(w_gate, GROUP_AXES, axis=0, tiled=True)
        full_up = lax.all_gather(w_up, GROUP_AXES, axis=0, tiled=True)
        cut = (share * 2 // 5) // 128 * 128
        full_down0 = lax.all_gather(w_down[:, :cut], GROUP_AXES, axis=0, tiled=False)
        full_down1 = lax.all_gather(w_down[:, cut:], GROUP_AXES, axis=0, tiled=False)

        x = hidden[0]
        normed = rms_norm(x.astype(F32), attn_gain)
        cos, sin = rope_tables(positions[0], head_dim)
        qkv = project_qkv(normed, full_qkv, cos, sin, heads + kv_heads)
        kv = qkv[:, heads * head_dim:]
        kv_peer = lax.ppermute(kv, 'cp', [(0, 1), (1, 0)])
        c = lax.axis_index('cp')
        table = jnp.where(c == 0, jnp.array([0, 2, 3, 1, 0, 3], jnp.int32), jnp.array([2, 0, 1, 3, 1, 2], jnp.int32))
        kv_all = jnp.concatenate([kv, kv_peer], axis=0)
        mixed = attention(qkv, kv_all, table, heads, kv_heads, head_dim)
        mid_own, normed_mlp = sum_over_tp(n_tp, mixed, full_out, x, attn_gain_row(mlp_gain), 0, True, 0)
        gate_proj = jnp.dot(normed_mlp, full_gate, preferred_element_type=F32)
        up_proj = jnp.dot(normed_mlp, full_up, preferred_element_type=F32)
        act = (jax.nn.silu(gate_proj) * up_proj).astype(BF16)
        piece0, = sum_over_tp(n_tp, act, full_down0, mid_own, attn_gain_row(mlp_gain), 0, False, 1)
        piece1, = sum_over_tp(n_tp, act, full_down1, mid_own, attn_gain_row(mlp_gain), cut, False, 2, after=(piece0,))
        return join_columns(piece0, piece1, n_w)[None]

    return jax.shard_map(layer_local, mesh=mesh, in_specs=(seq_spec, pos_spec, rep_spec, in_spec, in_spec, in_spec, out_spec, rep_spec, col_spec, col_spec, row_spec), out_specs=seq_spec, check_vma=False)


def attn_gain_row(gain):
    return gain[None, :]
```

time: 1510 us -> 1020 us (0.68)
  waiting for transfers between devices: 982 us -> 52.7 us
  Pallas kernels: 0 us -> 766 us
  matrix products: 382 us -> 139 us
  other arithmetic: 95.6 us -> 28.2 us
    pallas_call x0 -> x6, Pallas kernels: none -> 766 us  [the longest x3 576 us: sum_over_tp(): pl.pallas_call(functools.partial(sum_kernel, n_tp, col_off, with_norm, le...]
    psum x2 -> x0, waiting for transfers between devices: 543 us -> none  [the longest x1 272 us: layer_local(): down_proj = lax.psum(down_part, 'tp')]
    dot_general x29 -> x2, matrix products: 350 us -> 139 us  [the longest x1 71.8 us: layer_local(): up_proj = jnp.dot(normed_mlp, full_up, preferred_element_type=F32)]
    all_gather x1, waiting for transfers between devices: 153 us -> 0.02 us  [layer_local(): full_gate = lax.all_gather(w_gate, GROUP_AXES, axis=0, tiled=True)]
    all_gather x7 -> x4, waiting for transfers between devices: 181 us -> 50.5 us  [the longest x1 50.5 us: layer_local(): full_qkv = lax.all_gather(w_qkv, GROUP_AXES, axis=0, tiled=True)]
    all_gather x1, waiting for transfers between devices: 102 us -> 0.01 us  [layer_local(): full_up = lax.all_gather(w_up, GROUP_AXES, axis=0, tiled=True)]
    reduce_sum x12 -> x0, other arithmetic: 37.9 us -> none  [one_block(): row_sum = jnp.sum(probs, axis=-1)]
    unnamed x2 -> x0, matrix products: 32.2 us -> none
  transfers between devices with their start and end apart: 11 -> 7, of which waited for: 8 -> 1; matrix products, arithmetic and copies ran while one was open for 26% -> 17% of each run, Pallas kernels for 0% -> 56%
where the time goes in v1:
time: 1020 us
  Pallas kernels  766 us (75%)
  matrix products  139 us (14%)
  waiting for transfers between devices  52.7 us (5%)
  other arithmetic  28.2 us (3%)
  local copies, waits for them, and re-layouts  15 us (1%)
  between operations  13.9 us (1%)
    pallas_call x3, Pallas kernels, sum_over_tp(): pl.pallas_call(functools.partial(sum_kernel, n_tp, col_off, with_norm, le...  576 us
    pallas_call x1, Pallas kernels, attention(): pl.pallas_call(functools.partial(attn_kernel, group, head_dim, per_seg),...  144 us
    dot_general x1, matrix products, layer_local(): up_proj = jnp.dot(normed_mlp, full_up, preferred_element_type=F32)  71.8 us
    dot_general x1, matrix products, layer_local(): gate_proj = jnp.dot(normed_mlp, full_gate, preferred_element_type=F32)  67.5 us
    all_gather x1, waiting for transfers between devices, layer_local(): full_qkv = lax.all_gather(w_qkv, GROUP_AXES, axis=0, tiled=True)  50.5 us
    pallas_call x1, Pallas kernels, project_qkv(): pl.pallas_call(functools.partial(qkv_kernel, head_dim, rope_heads), grid=...  33.2 us
  transfers between devices with their start and end apart: 7, of which 1 were waited for; matrix products, arithmetic and copies ran while one was open for 17% of the time, Pallas kernels for 56%

profile of v1, /device:TPU:97, one launch (start us, length us, event | category | flops | bytes accessed | tf_op | source)
XLA Modules:
  0.0 1015.3 jit_solution(1501327036997396748)
XLA Ops:
  6.6 1.7 copy.20
  8.2 1.2 copy_bitcast_fusion.1
  9.4 1.4 pad_maximum_fusion.1
  10.9 0.1 all-gather.11.cloned.1.call-start
  10.9 0.7 all-gather.11.cloned.1.call-update
  11.7 0.1 all-gather.13.cloned.1.call-start
  11.8 0.7 all-gather.13.cloned.1.call-update
  12.5 0.1 all-gather.15.cloned.1.call-start
  12.6 0.6 all-gather.15.cloned.1.call-update
  13.1 0.1 all-gather.17.cloned.1.call-start
  13.2 2.9 slice.10
  16.1 0.1 all-gather.19.cloned.1.call-start
  16.3 7.3 fusion
  23.6 2.8 fusion.3
  26.4 1.7 pad_maximum_fusion.2
  28.1 14.7 %fusion.2.a_ref = bf16[1536,5120]{1,0:T(8,128)(2,1)} fusion(f32[5120]{0:T(1024)S(1)} %copy-done.2, f32[1536]{0:T(1024)S(1)} %add_rsqrt_fusion, bf16[1,1536,5120]{2,1,0:T(8,128)(2,1)} %param.13), kind=kLoop, calls=%fused_computation.4 | loop fusion | flops 31457280 | bytes 31483904 | tf_op jit(solution)/shard_map/convert_element_type | solution.py:23
  42.8 50.5 %all-gather.9.cloned.1.call-done.w_ref = bf16[5120,1536]{1,0:T(8,128)(2,1)} async-done(((bf16[640,1536]{1,0:T(8,128)(2,1)}), bf16[5120,1536]{1,0:T(8,128)(2,1)}) %all-gather.9.cloned.1.call-update) | async-done | bytes 15728656 | tf_op jit(solution)/shard_map/all_gather | solution.py:365
  93.3 33.2 %qkv.1.q_ref = bf16[1536,1536]{1,0:T(8,128)(2,1)} custom-call(bf16[1536,5120]{1,0:T(8,128)(2,1)} %fusion.2.a_ref, bf16[5120,1536]{1,0:T(8,128)(2,1)} %all-gather.9.cloned.1.call-done.w_ref, f32[1536,128]{1,0:T(8,128)} %get-tuple-element.14.cos_ref, f32[1536,128]{1,0:T(8,128)} %get-tuple-element.15.sin_ref), custom_call_target="tpu_custom_call" | custom-call | flops 24159191040 | bytes 36175872 | tf_op jit(solution)/shard_map/qkv/pallas_call | solution.py:50
  126.5 1.5 slice.12
  128.0 0.4 collective-permute-start
  128.4 3.6 slice.11
  132.1 0.1 all-gather.19.cloned.1.call-update
  132.2 0.2 pad_maximum_fusion.k_ref.v_ref
  132.4 2.4 copy-done
  134.8 143.9 %attn.1.lhs_hbm = bf16[1536,1024]{1,0:T(8,128)(2,1)S(1)} custom-call(s32[6]{0:T(128)S(1)} %broadcast_select_fusion.table_ref, bf16[1536,1536]{1,0:T(8,128)(2,1)S(1)} %copy-done, bf16[3072,512]{1,0:T(8,128)(2,1)S(1)} %pad_maximum_fusion.k_ref.v_ref, bf16[3072,512]{1,0:T(8,128)(2,1)S(1)} %pad_maximum_fusion.k_ref.v_ref), custom_call_target="tpu_custom_call" | custom-call | flops 19327352832 | bytes 9437184 | tf_op jit(solution)/shard_map/attn/pallas_call | solution.py:116
  278.8 1.7 copy-done.1
  280.4 269.4 %sum_tp_0.1 = (bf16[384,5120]{1,0:T(8,128)(2,1)}, bf16[1536,5120]{1,0:T(8,128)(2,1)}) custom-call(bf16[1536,1024]{1,0:T(8,128)(2,1)} %copy-done.1, bf16[8,1024,640]{2,1,0:T(8,128)(2,1)} %all-gather.11.cloned.1.call-done.w_hbm, bf16[1536,5120]{1,0:T(8,128)(2,1)} %bitcast.22, f32[1,5120]{1,0:T(1,128)} %bitcast.30), custom_call_target="tpu_custom_call" | custom-call | flops 471859200000 | bytes 45088768 | tf_op jit(solution)/shard_map/sum_tp_0/pallas_call | solution.py:314
  549.9 67.5 %fusion.4 = f32[1536,3584]{1,0:T(8,128)} fusion(bf16[1536,5120]{1,0:T(8,128)(2,1)} %get-tuple-element.7, bf16[5120,3584]{1,0:T(8,128)(2,1)} %all-gather.13.cloned.1.call-done), kind=kOutput, calls=%fused_computation.20 | convolution fusion | flops 56371445760 | bytes 74448896 | tf_op jit(solution)/shard_map/dot_general | solution.py:384
  617.3 71.8 %multiply_convert_fusion.lhs_hbm = bf16[1536,3584]{1,0:T(8,128)(2,1)} fusion(f32[1536,3584]{1,0:T(8,128)} %fusion.4, bf16[1536,5120]{1,0:T(8,128)(2,1)} %get-tuple-element.7, bf16[5120,3584]{1,0:T(8,128)(2,1)} %all-gather.15.cloned.1.call-done), kind=kOutput, calls=%fused_computation.5 | convolution fusion | flops 56404475904 | bytes 85458944 | tf_op jit(solution)/shard_map/dot_general | solution.py:385
  689.2 121.8 %sum_tp_1.1.refs_0_.a_ref = bf16[1536,2048]{1,0:T(8,128)(2,1)} custom-call(bf16[1536,3584]{1,0:T(8,128)(2,1)} %multiply_convert_fusion.lhs_hbm, bf16[8,3584,256]{2,1,0:T(8,128)(2,1)} %bitcast.29, bf16[384,5120]{1,0:T(8,128)(2,1)} %get-tuple-element.8.res_hbm, f32[1,5120]{1,0:T(1,128)} %bitcast.31), custom_call_target="tpu_custom_call" | custom-call | flops 188743680000 | bytes 38273024 | tf_op jit(solution)/shard_map/sum_tp_1/pallas_call | solution.py:314
  811.0 184.9 %sum_tp_2.1.b_ref = bf16[1536,3072]{1,0:T(8,128)(2,1)} custom-call(bf16[1536,3584]{1,0:T(8,128)(2,1)} %multiply_convert_fusion.lhs_hbm, bf16[8,3584,384]{2,1,0:T(8,128)(2,1)} %bitcast.28, bf16[384,5120]{1,0:T(8,128)(2,1)} %get-tuple-element.8.res_hbm, f32[1,5120]{1,0:T(1,128)} %bitcast.32, bf16[1536,2048]{1,0:T(8,128)(2,1)} %sum_tp_1.1.refs_0_.a_ref), custom_call_target="tpu_custom_call" | custom-call | flops 283115520000 | bytes 51904512 | tf_op jit(solution)/shard_map/sum_tp_2/pallas_call | solution.py:314
  995.9 12.3 %join.1 = bf16[1536,5120]{1,0:T(8,128)(2,1)} custom-call(bf16[1536,2048]{1,0:T(8,128)(2,1)} %sum_tp_1.1.refs_0_.a_ref, bf16[1536,3072]{1,0:T(8,128)(2,1)} %sum_tp_2.1.b_ref), custom_call_target="tpu_custom_call" | custom-call | flops 7864320 | bytes 31457280 | tf_op jit(solution)/shard_map/join/pallas_call | solution.py:338
  (23 shorter events, 0.2 us)
Async XLA Ops:
  6.5 9.7 copy-start.3
  6.5 86.8 %all-gather.9.cloned.1.call-start = ((), (), s32[]{:S(2)}) async-start(), calls=%async_computation | async-start | bytes 17694720 | tf_op jit(solution)/shard_map/all_gather | solution.py:365
  10.9 269.6 %all-gather.11.cloned.1.call-start = ((), (), s32[]{:S(2)}) async-start(), calls=%async_computation.1 | async-start | bytes 11796480 | tf_op jit(solution)/shard_map/all_gather | solution.py:366
  11.7 538.2 %all-gather.13.cloned.1.call-start = ((), (), s32[]{:S(2)}) async-start(), calls=%async_computation.2 | async-start | bytes 41287680 | tf_op jit(solution)/shard_map/all_gather | solution.py:367
  12.5 15.6 %copy-start.2 = (f32[5120]{0:T(1024)S(1)}, f32[5120]{0:T(1024)}, u32[]{:S(2)}) copy-start(f32[5120]{0:T(1024)} %param.15) | copy-start | bytes 61444
  12.5 604.9 %all-gather.15.cloned.1.call-start = ((), (), s32[]{:S(2)}) async-start(), calls=%async_computation.3 | async-start | bytes 41287680 | tf_op jit(solution)/shard_map/all_gather | solution.py:368
  13.1 676.0 %all-gather.17.cloned.1.call-start = ((), (), s32[]{:S(2)}) async-start(), calls=%async_computation.4 | async-start | bytes 16515072 | tf_op jit(solution)/shard_map/all_gather | solution.py:370
  16.1 794.8 %all-gather.19.cloned.1.call-start = ((), (), s32[]{:S(2)}) async-start(), calls=%async_computation.5 | async-start | bytes 24772608 | tf_op jit(solution)/shard_map/all_gather | solution.py:371
  93.3 38.9 %copy-start.4 = (s32[6]{0:T(128)S(1)}, s32[6]{0:T(128)}, u32[]{:S(2)}) copy-start(s32[6]{0:T(128)} %constant.27.clone) | copy-start | bytes 76
  93.3 38.9 %copy-start.5 = (s32[6]{0:T(128)S(1)}, s32[6]{0:T(128)}, u32[]{:S(2)}) copy-start(s32[6]{0:T(128)} %constant.28.clone) | copy-start | bytes 76
  128.0 4.1 collective-permute-start
  132.4 2.4 copy-start
  278.8 1.7 copy-start.1
Sparse Core Ops, SparseCore 0:
  11.0 82.2 all-gather.8
  94.9 56.4 all-gather.10
  153.0 168.5 all-gather.12
  323.1 167.4 all-gather.14
  492.0 72.6 all-gather.16
  566.2 104.8 all-gather.18

commit v2 on v1

--- a/solution.py
+++ b/solution.py
@@ -64,7 +64,7 @@
     )(a, w, cos, sin)
 
 
-def attn_kernel(group, head_dim, per_seg, table_ref, q_ref, k_ref, v_ref, o_ref, m_sc, l_sc, acc_sc):
+def attn_kernel(group, head_dim, per_seg, table_ref, q_ref, k_ref, vt_ref, o_ref, m_sc, l_sc, acc_sc):
     blk = q_ref.shape[0]
     seg_rows = per_seg * blk
     qi = pl.program_id(1)
@@ -78,23 +78,20 @@
     def step(j, masked):
         row = table_ref[j // per_seg] * seg_rows + lax.rem(j, per_seg) * blk
         rows = pl.ds(pl.multiple_of(row, blk), blk)
-        k, v = k_ref[rows, :], v_ref[rows, :]
+        k, vt = k_ref[rows, :], vt_ref[:, rows]
         for h in range(group):
             q = q_ref[:, h * head_dim:(h + 1) * head_dim]
-            s = lax.dot_general(q, k, (((1,), (1,)), ((), ())), preferred_element_type=F32)
+            s = lax.dot_general(k, q, (((1,), (1,)), ((), ())), preferred_element_type=F32) * scale
             if masked:
-                keep = lax.broadcasted_iota(jnp.int32, s.shape, 0) >= lax.broadcasted_iota(jnp.int32, s.shape, 1)
+                keep = lax.broadcasted_iota(jnp.int32, s.shape, 0) <= lax.broadcasted_iota(jnp.int32, s.shape, 1)
                 s = jnp.where(keep, s, -1e30)
-            m_old = m_sc[h, :, 0:1]
-            m_new = jnp.maximum(m_old, jnp.max(s, axis=1, keepdims=True))
-            alpha = jnp.exp2((m_old - m_new) * scale)
-            p = jnp.exp2((s - m_new) * scale)
-            part = p[:, 0:128]
-            for c in range(128, blk, 128):
-                part = part + p[:, c:c + 128]
-            l_sc[h] = l_sc[h] * alpha + part
-            acc_sc[h] = acc_sc[h] * alpha + jnp.dot(p.astype(BF16), v, preferred_element_type=F32)
-            m_sc[h] = jnp.broadcast_to(m_new, m_sc.shape[1:])
+            m_old = m_sc[h]
+            m_new = jnp.maximum(m_old, jnp.max(s, axis=0, keepdims=True))
+            alpha = jnp.exp2(m_old - m_new)
+            p = jnp.exp2(s - m_new)
+            l_sc[h] = l_sc[h] * alpha + jnp.sum(p, axis=0, keepdims=True)
+            acc_sc[h] = acc_sc[h] * alpha + jnp.dot(vt, p.astype(BF16), preferred_element_type=F32)
+            m_sc[h] = m_new
 
     def body(j, carry):
         step(j, False)
@@ -103,12 +100,11 @@
     lax.fori_loop(0, n_full, body, 0)
     step(n_full, True)
     for h in range(group):
-        total = jnp.sum(l_sc[h], axis=1, keepdims=True)
-        o_ref[:, h * head_dim:(h + 1) * head_dim] = (acc_sc[h] / total).astype(BF16)
-
-
-def attention(qkv, kv_all, table, heads, kv_heads, head_dim):
-    tokens, keys = qkv.shape[0], kv_all.shape[0]
+        o_ref[:, h * head_dim:(h + 1) * head_dim] = (acc_sc[h] / l_sc[h]).T.astype(BF16)
+
+
+def attention(qkv, k_all, vt_all, table, heads, kv_heads, head_dim):
+    tokens, keys = qkv.shape[0], k_all.shape[0]
     seg_rows = tokens // 2
     blk = min(256, seg_rows)
     per_seg = seg_rows // blk
@@ -121,16 +117,16 @@
             in_specs=[
                 pl.BlockSpec((blk, group * head_dim), lambda g, i, t: (i, g)),
                 pl.BlockSpec((keys, head_dim), lambda g, i, t: (0, g)),
-                pl.BlockSpec((keys, head_dim), lambda g, i, t: (0, kv_heads + g)),
+                pl.BlockSpec((head_dim, keys), lambda g, i, t: (g, 0)),
             ],
             out_specs=pl.BlockSpec((blk, group * head_dim), lambda g, i, t: (i, g)),
-            scratch_shapes=[pltpu.VMEM((group, blk, 128), F32), pltpu.VMEM((group, blk, 128), F32), pltpu.VMEM((group, blk, head_dim), F32)],
+            scratch_shapes=[pltpu.VMEM((group, 1, blk), F32), pltpu.VMEM((group, 1, blk), F32), pltpu.VMEM((group, head_dim, blk), F32)],
         ),
         out_shape=jax.ShapeDtypeStruct((tokens, heads * head_dim), BF16),
         compiler_params=pltpu.CompilerParams(vmem_limit_bytes=32 * 1024 * 1024),
         cost_estimate=pl.CostEstimate(flops=2 * tokens * keys * heads * head_dim * 2, bytes_accessed=2 * (2 * tokens * heads * head_dim + 4 * keys * head_dim), transcendentals=tokens * keys * heads),
         name="attn",
-    )(table, qkv, kv_all, kv_all)
+    )(table, qkv, k_all, vt_all)
 
 
 def sum_kernel(n_tp, col_off, with_norm, n_after, lhs_hbm, w_hbm, res_hbm, gain_ref, *refs):
@@ -379,7 +375,8 @@
         c = lax.axis_index('cp')
         table = jnp.where(c == 0, jnp.array([0, 2, 3, 1, 0, 3], jnp.int32), jnp.array([2, 0, 1, 3, 1, 2], jnp.int32))
         kv_all = jnp.concatenate([kv, kv_peer], axis=0)
-        mixed = attention(qkv, kv_all, table, heads, kv_heads, head_dim)
+        k_all, vt_all = kv_all[:, :kv_heads * head_dim], kv_all[:, kv_heads * head_dim:].T
+        mixed = attention(qkv, k_all, vt_all, table, heads, kv_heads, head_dim)
         mid_own, normed_mlp = sum_over_tp(n_tp, mixed, full_out, x, attn_gain_row(mlp_gain), 0, True, 0)
         gate_proj = jnp.dot(normed_mlp, full_gate, preferred_element_type=F32)
         up_proj = jnp.dot(normed_mlp, full_up, preferred_element_type=F32)

time: 1020 us -> 989 us (0.970)
  Pallas kernels: 766 us -> 724 us
    pallas_call x1, Pallas kernels: 144 us -> 102 us  [attention(): pl.pallas_call(functools.partial(attn_kernel, group, head_dim, per_seg),...]
  transfers between devices with their start and end apart: 7 -> 7, of which waited for: 1 -> 1; matrix products, arithmetic and copies ran while one was open for 17% -> 18% of each run, Pallas kernels for 56% -> 54%
where the time goes in v2:
time: 989 us; the launch traced here: 979 us
  Pallas kernels  724 us (73%)
  matrix products  140 us (14%)
  waiting for transfers between devices  52.7 us (5%)
  other arithmetic  30.7 us (3%)
  local copies, waits for them, and re-layouts  17.4 us (2%)
  between operations  13.9 us (1%)
    pallas_call x3, Pallas kernels, sum_over_tp(): pl.pallas_call(functools.partial(sum_kernel, n_tp, col_off, with_norm, le...  577 us
    pallas_call x1, Pallas kernels, attention(): pl.pallas_call(functools.partial(attn_kernel, group, head_dim, per_seg),...  102 us
    dot_general x1, matrix products, layer_local(): up_proj = jnp.dot(normed_mlp, full_up, preferred_element_type=F32)  71.8 us
    dot_general x1, matrix products, layer_local(): gate_proj = jnp.dot(normed_mlp, full_gate, preferred_element_type=F32)  67.8 us
    all_gather x1, waiting for transfers between devices, layer_local(): full_qkv = lax.all_gather(w_qkv, GROUP_AXES, axis=0, tiled=True)  50.5 us
    pallas_call x1, Pallas kernels, project_qkv(): pl.pallas_call(functools.partial(qkv_kernel, head_dim, rope_heads), grid=...  33.2 us
  transfers between devices with their start and end apart: 7, of which 1 were waited for; matrix products, arithmetic and copies ran while one was open for 18% of the time, Pallas kernels for 54%

profile of v2, /device:TPU:97, one launch (start us, length us, event | category | flops | bytes accessed | tf_op | source)
XLA Modules:
  0.0 979.4 jit_solution(6197013654121951965)
XLA Ops:
  6.6 1.7 copy.25
  8.2 1.2 copy_bitcast_fusion.1
  9.4 1.4 pad_maximum_fusion
  10.9 0.1 all-gather.11.cloned.1.call-start
  10.9 0.7 all-gather.11.cloned.1.call-update
  11.8 0.7 all-gather.13.cloned.1.call-update
  12.5 0.1 all-gather.15.cloned.1.call-start
  12.5 0.6 all-gather.15.cloned.1.call-update
  13.1 0.1 all-gather.17.cloned.1.call-start
  13.2 2.9 slice.18
  16.1 0.1 all-gather.19.cloned.1.call-start
  16.3 7.3 fusion
  23.6 2.8 fusion.5
  26.5 1.7 pad_maximum_fusion.2
  28.1 14.7 %fusion.2.a_ref = bf16[1536,5120]{1,0:T(8,128)(2,1)} fusion(f32[5120]{0:T(1024)S(1)} %copy-done.2, f32[1536]{0:T(1024)S(1)} %add_rsqrt_fusion, bf16[1,1536,5120]{2,1,0:T(8,128)(2,1)} %param.13), kind=kLoop, calls=%fused_computation.4 | loop fusion | flops 31457280 | bytes 31483904 | tf_op jit(solution)/shard_map/convert_element_type | solution.py:23
  42.8 50.5 %all-gather.9.cloned.1.call-done.w_ref = bf16[5120,1536]{1,0:T(8,128)(2,1)} async-done(((bf16[640,1536]{1,0:T(8,128)(2,1)}), bf16[5120,1536]{1,0:T(8,128)(2,1)}) %all-gather.9.cloned.1.call-update) | async-done | bytes 15728656 | tf_op jit(solution)/shard_map/all_gather | solution.py:361
  93.3 33.2 %qkv.1.q_ref = bf16[1536,1536]{1,0:T(8,128)(2,1)} custom-call(bf16[1536,5120]{1,0:T(8,128)(2,1)} %fusion.2.a_ref, bf16[5120,1536]{1,0:T(8,128)(2,1)} %all-gather.9.cloned.1.call-done.w_ref, f32[1536,128]{1,0:T(8,128)} %get-tuple-element.16.cos_ref, f32[1536,128]{1,0:T(8,128)} %get-tuple-element.17.sin_ref), custom_call_target="tpu_custom_call" | custom-call | flops 24159191040 | bytes 36175872 | tf_op jit(solution)/shard_map/qkv/pallas_call | solution.py:50
  126.5 1.5 slice.20
  128.1 0.7 copy.18
  128.8 0.4 collective-permute-start
  129.2 3.6 slice.19
  132.9 2.8 fusion.4
  135.7 1.7 copy.17.k_ref
  137.4 2.4 copy-done
  139.8 101.8 %attn.1.lhs_hbm = bf16[1536,1024]{1,0:T(8,128)(2,1)S(1)} custom-call(s32[6]{0:T(128)S(1)} %broadcast_select_fusion.table_ref, bf16[1536,1536]{1,0:T(8,128)(2,1)S(1)} %copy-done, bf16[3072,256]{1,0:T(8,128)(2,1)S(1)} %copy.17.k_ref, bf16[256,3072]{1,0:T(8,128)(2,1)S(1)} %get-tuple-element.9.vt_ref), custom_call_target="tpu_custom_call" | custom-call | flops 19327352832 | bytes 9437184 | tf_op jit(solution)/shard_map/attn/pallas_call | solution.py:112
  241.6 1.7 copy-done.1
  243.3 269.3 %sum_tp_0.1 = (bf16[384,5120]{1,0:T(8,128)(2,1)}, bf16[1536,5120]{1,0:T(8,128)(2,1)}) custom-call(bf16[1536,1024]{1,0:T(8,128)(2,1)} %copy-done.1, bf16[8,1024,640]{2,1,0:T(8,128)(2,1)} %all-gather.11.cloned.1.call-done.w_hbm, bf16[1536,5120]{1,0:T(8,128)(2,1)} %bitcast.24, f32[1,5120]{1,0:T(1,128)} %bitcast.32), custom_call_target="tpu_custom_call" | custom-call | flops 471859200000 | bytes 45088768 | tf_op jit(solution)/shard_map/sum_tp_0/pallas_call | solution.py:310
  512.6 67.8 %fusion.6 = f32[1536,3584]{1,0:T(8,128)} fusion(bf16[1536,5120]{1,0:T(8,128)(2,1)} %get-tuple-element.7, bf16[5120,3584]{1,0:T(8,128)(2,1)} %all-gather.13.cloned.1.call-done), kind=kOutput, calls=%fused_computation.24 | convolution fusion | flops 56371445760 | bytes 74448896 | tf_op jit(solution)/shard_map/dot_general | solution.py:381
  580.4 71.8 %multiply_convert_fusion.lhs_hbm = bf16[1536,3584]{1,0:T(8,128)(2,1)} fusion(f32[1536,3584]{1,0:T(8,128)} %fusion.6, bf16[1536,5120]{1,0:T(8,128)(2,1)} %get-tuple-element.7, bf16[5120,3584]{1,0:T(8,128)(2,1)} %all-gather.15.cloned.1.call-done), kind=kOutput, calls=%fused_computation.5 | convolution fusion | flops 56404475904 | bytes 85458944 | tf_op jit(solution)/shard_map/dot_general | solution.py:382
  652.2 122.8 %sum_tp_1.1.refs_0_.a_ref = bf16[1536,2048]{1,0:T(8,128)(2,1)} custom-call(bf16[1536,3584]{1,0:T(8,128)(2,1)} %multiply_convert_fusion.lhs_hbm, bf16[8,3584,256]{2,1,0:T(8,128)(2,1)} %bitcast.31, bf16[384,5120]{1,0:T(8,128)(2,1)} %get-tuple-element.8.res_hbm, f32[1,5120]{1,0:T(1,128)} %bitcast.33), custom_call_target="tpu_custom_call" | custom-call | flops 188743680000 | bytes 38273024 | tf_op jit(solution)/shard_map/sum_tp_1/pallas_call | solution.py:310
  775.0 185.0 %sum_tp_2.1.b_ref = bf16[1536,3072]{1,0:T(8,128)(2,1)} custom-call(bf16[1536,3584]{1,0:T(8,128)(2,1)} %multiply_convert_fusion.lhs_hbm, bf16[8,3584,384]{2,1,0:T(8,128)(2,1)} %bitcast.30, bf16[384,5120]{1,0:T(8,128)(2,1)} %get-tuple-element.8.res_hbm, f32[1,5120]{1,0:T(1,128)} %bitcast.34, bf16[1536,2048]{1,0:T(8,128)(2,1)} %sum_tp_1.1.refs_0_.a_ref), custom_call_target="tpu_custom_call" | custom-call | flops 283115520000 | bytes 51904512 | tf_op jit(solution)/shard_map/sum_tp_2/pallas_call | solution.py:310
  960.1 12.3 %join.1 = bf16[1536,5120]{1,0:T(8,128)(2,1)} custom-call(bf16[1536,2048]{1,0:T(8,128)(2,1)} %sum_tp_1.1.refs_0_.a_ref, bf16[1536,3072]{1,0:T(8,128)(2,1)} %sum_tp_2.1.b_ref), custom_call_target="tpu_custom_call" | custom-call | flops 7864320 | bytes 31457280 | tf_op jit(solution)/shard_map/join/pallas_call | solution.py:334
  (25 shorter events, 0.3 us)
Async XLA Ops:
  6.5 86.8 %all-gather.9.cloned.1.call-start = ((), (), s32[]{:S(2)}) async-start(), calls=%async_computation | async-start | bytes 17694720 | tf_op jit(solution)/shard_map/all_gather | solution.py:361
  10.8 5.4 copy-start.3
  10.9 232.4 %all-gather.11.cloned.1.call-start = ((), (), s32[]{:S(2)}) async-start(), calls=%async_computation.1 | async-start | bytes 11796480 | tf_op jit(solution)/shard_map/all_gather | solution.py:362
  11.7 500.9 %all-gather.13.cloned.1.call-start = ((), (), s32[]{:S(2)}) async-start(), calls=%async_computation.2 | async-start | bytes 41287680 | tf_op jit(solution)/shard_map/all_gather | solution.py:363
  12.5 567.9 %all-gather.15.cloned.1.call-start = ((), (), s32[]{:S(2)}) async-start(), calls=%async_computation.3 | async-start | bytes 41287680 | tf_op jit(solution)/shard_map/all_gather | solution.py:364
  13.1 639.0 %all-gather.17.cloned.1.call-start = ((), (), s32[]{:S(2)}) async-start(), calls=%async_computation.4 | async-start | bytes 16515072 | tf_op jit(solution)/shard_map/all_gather | solution.py:366
  16.1 758.9 %all-gather.19.cloned.1.call-start = ((), (), s32[]{:S(2)}) async-start(), calls=%async_computation.5 | async-start | bytes 24772608 | tf_op jit(solution)/shard_map/all_gather | solution.py:367
  16.3 11.9 %copy-start.2 = (f32[5120]{0:T(1024)S(1)}, f32[5120]{0:T(1024)}, u32[]{:S(2)}) copy-start(f32[5120]{0:T(1024)} %param.15) | copy-start | bytes 61444
  126.5 6.3 copy-start.4
  126.5 6.4 copy-start.5
  128.8 4.1 collective-permute-start
  137.4 2.4 copy-start
  241.6 1.7 copy-start.1
Sparse Core Ops, SparseCore 0:
  11.0 82.2 all-gather.8
  94.9 56.4 all-gather.10
  153.0 168.5 all-gather.12
  323.1 167.3 all-gather.14
  491.9 72.6 all-gather.16
  566.0 104.8 all-gather.18

commit v3 on v2

--- a/solution.py
+++ b/solution.py
@@ -10,7 +10,7 @@
 ROPE_THETA = 500000.0
 NORM_EPS = 1e-5
 GROUP_AXES = ('fsdp', 'cp')
-N_SUB = 4
+N_SUB = 6
 F32 = jnp.float32
 BF16 = jnp.bfloat16
 MESH = pl.DeviceIdType.MESH
@@ -69,21 +69,20 @@
     seg_rows = per_seg * blk
     qi = pl.program_id(1)
     true_seg = table_ref[4 + qi // per_seg]
-    n_full = true_seg * per_seg + lax.rem(qi, per_seg)
+    within = lax.rem(qi, per_seg) * blk
     scale = (head_dim ** -0.5) * 1.4426950408889634
     m_sc[...] = jnp.full(m_sc.shape, -1e30, F32)
     l_sc[...] = jnp.zeros(l_sc.shape, F32)
     acc_sc[...] = jnp.zeros(acc_sc.shape, F32)
 
     def step(j, masked):
-        row = table_ref[j // per_seg] * seg_rows + lax.rem(j, per_seg) * blk
-        rows = pl.ds(pl.multiple_of(row, blk), blk)
+        rows = pl.ds(pl.multiple_of(table_ref[j] * seg_rows, seg_rows), seg_rows)
         k, vt = k_ref[rows, :], vt_ref[:, rows]
         for h in range(group):
             q = q_ref[:, h * head_dim:(h + 1) * head_dim]
             s = lax.dot_general(k, q, (((1,), (1,)), ((), ())), preferred_element_type=F32) * scale
             if masked:
-                keep = lax.broadcasted_iota(jnp.int32, s.shape, 0) <= lax.broadcasted_iota(jnp.int32, s.shape, 1)
+                keep = lax.broadcasted_iota(jnp.int32, s.shape, 0) <= lax.broadcasted_iota(jnp.int32, s.shape, 1) + within
                 s = jnp.where(keep, s, -1e30)
             m_old = m_sc[h]
             m_new = jnp.maximum(m_old, jnp.max(s, axis=0, keepdims=True))
@@ -97,8 +96,8 @@
         step(j, False)
         return carry
 
-    lax.fori_loop(0, n_full, body, 0)
-    step(n_full, True)
+    lax.fori_loop(0, true_seg, body, 0)
+    step(true_seg, True)
     for h in range(group):
         o_ref[:, h * head_dim:(h + 1) * head_dim] = (acc_sc[h] / l_sc[h]).T.astype(BF16)
 
@@ -193,11 +192,14 @@
         return remote(where, where, s4.at[s, i], r4.at[s, i], sides[i])
 
     def stage_a(s):
-        left_rows = lhs[:, s * rows:(s + 1) * rows, :].reshape(n_tp * rows, depth)
+        at = pl.ds(pl.multiple_of(s * rows, rows), rows)
 
         def one(d, carry):
-            if s == 0:
+            @pl.when(s == 0)
+            def _():
                 w_copy(d).wait()
+
+            left_rows = lhs[:, at, :].reshape(n_tp * rows, depth)
             prod = jnp.dot(left_rows, w[d], preferred_element_type=F32).astype(BF16)
             part[s, :, :, pl.ds(pl.multiple_of(d * n_cols, n_cols), n_cols)] = prod.reshape(n_tp, rows, n_cols)
             return carry
@@ -244,7 +246,7 @@
         return pltpu.make_async_copy(norm.at[s], out_hbm.at[rows_of(me, s), :], o_sem.at[s, 0])
 
     def keep(s):
-        return pltpu.make_async_copy(own.at[s], own_hbm.at[pl.ds(s * rows, rows), :], o_sem.at[s, 1])
+        return pltpu.make_async_copy(own.at[s], own_hbm.at[pl.ds(pl.multiple_of(s * rows, rows), rows), :], o_sem.at[s, 1])
 
     def arrive3(s, i):
         where = out_hbm.at[rows_of(sides[1 - i], s), :]
@@ -261,19 +263,34 @@
 
     for c in lhs_copies:
         c.wait()
-    for t in range(N_SUB + 3):
-        if t < N_SUB:
+
+    def tick(t, carry):
+        @pl.when(t < N_SUB)
+        def _():
             stage_a(t)
-        if 0 <= t - 1 < N_SUB:
+
+        @pl.when((t >= 1) & (t < N_SUB + 1))
+        def _():
             stage_b(t - 1)
-        if t == 1:
+
+        @pl.when(t == 1)
+        def _():
             for c in res_copies:
                 c.wait()
-        if 0 <= t - 2 < N_SUB:
+
+        @pl.when((t >= 2) & (t < N_SUB + 2))
+        def _():
             stage_c(t - 2)
-        if 0 <= t - 3 < N_SUB:
+
+        @pl.when(t >= 3)
+        def _():
             stage_d(t - 3)
-    for s in range(N_SUB):
+
+        return carry
+
+    lax.fori_loop(0, N_SUB + 3, tick, 0)
+
+    def drain(s, carry):
         local(s).wait()
         if with_norm:
             keep(s).wait()
@@ -283,6 +300,9 @@
             hop3(s, i).wait_send()
             hop4(s, i).wait_send()
             arrive4(s, i).wait_recv()
+        return carry
+
+    lax.fori_loop(0, N_SUB, drain, 0)
 
 
 def sum_over_tp(n_tp, lhs, w, res, gain, col_off, with_norm, collective_id, after=()):

time: 989 us -> 936 us (0.946)
  Pallas kernels: 724 us -> 681 us
    pallas_call x1, Pallas kernels: 102 us -> 68.9 us  [attention(): pl.pallas_call(functools.partial(attn_kernel, group, head_dim, per_seg),...]
    pallas_call x3, Pallas kernels: 577 us -> 567 us  [sum_over_tp(): pl.pallas_call(functools.partial(sum_kernel, n_tp, col_off, with_norm, le...]
  transfers between devices with their start and end apart: 7 -> 7, of which waited for: 1 -> 1; matrix products, arithmetic and copies ran while one was open for 18% -> 19% of each run, Pallas kernels for 54% -> 52%
where the time goes in v3:
time: 936 us; the launch traced here: 935 us
  Pallas kernels  681 us (73%)
  matrix products  139 us (15%)
  waiting for transfers between devices  52.7 us (6%)
  other arithmetic  30.7 us (3%)
  local copies, waits for them, and re-layouts  17.4 us (2%)
  between operations  13.7 us (1%)
    pallas_call x3, Pallas kernels, sum_over_tp(): pl.pallas_call(functools.partial(sum_kernel, n_tp, col_off, with_norm, le...  567 us
    dot_general x1, matrix products, layer_local(): up_proj = jnp.dot(normed_mlp, full_up, preferred_element_type=F32)  71.6 us
    pallas_call x1, Pallas kernels, attention(): pl.pallas_call(functools.partial(attn_kernel, group, head_dim, per_seg),...  68.9 us
    dot_general x1, matrix products, layer_local(): gate_proj = jnp.dot(normed_mlp, full_gate, preferred_element_type=F32)  67.3 us
    all_gather x1, waiting for transfers between devices, layer_local(): full_qkv = lax.all_gather(w_qkv, GROUP_AXES, axis=0, tiled=True)  50.5 us
    pallas_call x1, Pallas kernels, project_qkv(): pl.pallas_call(functools.partial(qkv_kernel, head_dim, rope_heads), grid=...  33.2 us
  transfers between devices with their start and end apart: 7, of which 1 were waited for; matrix products, arithmetic and copies ran while one was open for 19% of the time, Pallas kernels for 52%

profile of v3, /device:TPU:97, one launch (start us, length us, event | category | flops | bytes accessed | tf_op | source)
XLA Modules:
  0.0 935.2 jit_solution(9328839809903453426)
XLA Ops:
  6.6 1.7 copy.25
  8.2 1.2 copy_bitcast_fusion.1
  9.4 1.4 pad_maximum_fusion
  10.9 0.1 all-gather.11.cloned.1.call-start
  10.9 0.7 all-gather.11.cloned.1.call-update
  11.7 0.1 all-gather.13.cloned.1.call-start
  11.8 0.7 all-gather.13.cloned.1.call-update
  12.5 0.6 all-gather.15.cloned.1.call-update
  13.1 0.1 all-gather.17.cloned.1.call-start
  13.2 2.9 slice.18
  16.1 0.1 all-gather.19.cloned.1.call-start
  16.3 7.3 fusion
  23.6 2.8 fusion.5
  26.5 1.7 pad_maximum_fusion.2
  28.1 14.7 %fusion.2.a_ref = bf16[1536,5120]{1,0:T(8,128)(2,1)} fusion(f32[5120]{0:T(1024)S(1)} %copy-done.2, f32[1536]{0:T(1024)S(1)} %add_rsqrt_fusion, bf16[1,1536,5120]{2,1,0:T(8,128)(2,1)} %param.13), kind=kLoop, calls=%fused_computation.4 | loop fusion | flops 31457280 | bytes 31483904 | tf_op jit(solution)/shard_map/convert_element_type | solution.py:23
  42.8 50.5 %all-gather.9.cloned.1.call-done.w_ref = bf16[5120,1536]{1,0:T(8,128)(2,1)} async-done(((bf16[640,1536]{1,0:T(8,128)(2,1)}), bf16[5120,1536]{1,0:T(8,128)(2,1)}) %all-gather.9.cloned.1.call-update) | async-done | bytes 15728656 | tf_op jit(solution)/shard_map/all_gather | solution.py:381
  93.3 33.2 %qkv.1.q_ref = bf16[1536,1536]{1,0:T(8,128)(2,1)} custom-call(bf16[1536,5120]{1,0:T(8,128)(2,1)} %fusion.2.a_ref, bf16[5120,1536]{1,0:T(8,128)(2,1)} %all-gather.9.cloned.1.call-done.w_ref, f32[1536,128]{1,0:T(8,128)} %get-tuple-element.16.cos_ref, f32[1536,128]{1,0:T(8,128)} %get-tuple-element.17.sin_ref), custom_call_target="tpu_custom_call" | custom-call | flops 24159191040 | bytes 36175872 | tf_op jit(solution)/shard_map/qkv/pallas_call | solution.py:50
  126.5 1.5 slice.20
  128.1 0.7 copy.18
  128.8 0.4 collective-permute-start
  129.2 3.6 slice.19
  132.9 2.8 fusion.4
  135.7 1.7 copy.17.k_ref
  137.4 2.4 copy-done
  139.8 68.9 %attn.1.lhs_hbm = bf16[1536,1024]{1,0:T(8,128)(2,1)S(1)} custom-call(s32[6]{0:T(128)S(1)} %broadcast_select_fusion.table_ref, bf16[1536,1536]{1,0:T(8,128)(2,1)S(1)} %copy-done, bf16[3072,256]{1,0:T(8,128)(2,1)S(1)} %copy.17.k_ref, bf16[256,3072]{1,0:T(8,128)(2,1)S(1)} %get-tuple-element.9.vt_ref), custom_call_target="tpu_custom_call" | custom-call | flops 19327352832 | bytes 9437184 | tf_op jit(solution)/shard_map/attn/pallas_call | solution.py:111
  208.8 1.7 copy-done.1
  210.4 267.3 %sum_tp_0.1 = (bf16[384,5120]{1,0:T(8,128)(2,1)}, bf16[1536,5120]{1,0:T(8,128)(2,1)}) custom-call(bf16[1536,1024]{1,0:T(8,128)(2,1)} %copy-done.1, bf16[8,1024,640]{2,1,0:T(8,128)(2,1)} %all-gather.11.cloned.1.call-done.w_hbm, bf16[1536,5120]{1,0:T(8,128)(2,1)} %bitcast.24, f32[1,5120]{1,0:T(1,128)} %bitcast.32), custom_call_target="tpu_custom_call" | custom-call | flops 471859200000 | bytes 45088768 | tf_op jit(solution)/shard_map/sum_tp_0/pallas_call | solution.py:330
  477.7 67.3 %fusion.6 = f32[1536,3584]{1,0:T(8,128)} fusion(bf16[1536,5120]{1,0:T(8,128)(2,1)} %get-tuple-element.7, bf16[5120,3584]{1,0:T(8,128)(2,1)} %all-gather.13.cloned.1.call-done), kind=kOutput, calls=%fused_computation.24 | convolution fusion | flops 56371445760 | bytes 74448896 | tf_op jit(solution)/shard_map/dot_general | solution.py:401
  545.0 71.6 %multiply_convert_fusion.lhs_hbm = bf16[1536,3584]{1,0:T(8,128)(2,1)} fusion(f32[1536,3584]{1,0:T(8,128)} %fusion.6, bf16[1536,5120]{1,0:T(8,128)(2,1)} %get-tuple-element.7, bf16[5120,3584]{1,0:T(8,128)(2,1)} %all-gather.15.cloned.1.call-done), kind=kOutput, calls=%fused_computation.5 | convolution fusion | flops 56404475904 | bytes 85458944 | tf_op jit(solution)/shard_map/dot_general | solution.py:402
  616.6 120.0 %sum_tp_1.1.refs_0_.a_ref = bf16[1536,2048]{1,0:T(8,128)(2,1)} custom-call(bf16[1536,3584]{1,0:T(8,128)(2,1)} %multiply_convert_fusion.lhs_hbm, bf16[8,3584,256]{2,1,0:T(8,128)(2,1)} %bitcast.31, bf16[384,5120]{1,0:T(8,128)(2,1)} %get-tuple-element.8.res_hbm, f32[1,5120]{1,0:T(1,128)} %bitcast.33), custom_call_target="tpu_custom_call" | custom-call | flops 188743680000 | bytes 38273024 | tf_op jit(solution)/shard_map/sum_tp_1/pallas_call | solution.py:330
  736.6 179.5 %sum_tp_2.1.b_ref = bf16[1536,3072]{1,0:T(8,128)(2,1)} custom-call(bf16[1536,3584]{1,0:T(8,128)(2,1)} %multiply_convert_fusion.lhs_hbm, bf16[8,3584,384]{2,1,0:T(8,128)(2,1)} %bitcast.30, bf16[384,5120]{1,0:T(8,128)(2,1)} %get-tuple-element.8.res_hbm, f32[1,5120]{1,0:T(1,128)} %bitcast.34, bf16[1536,2048]{1,0:T(8,128)(2,1)} %sum_tp_1.1.refs_0_.a_ref), custom_call_target="tpu_custom_call" | custom-call | flops 283115520000 | bytes 51904512 | tf_op jit(solution)/shard_map/sum_tp_2/pallas_call | solution.py:330
  916.1 12.3 %join.1 = bf16[1536,5120]{1,0:T(8,128)(2,1)} custom-call(bf16[1536,2048]{1,0:T(8,128)(2,1)} %sum_tp_1.1.refs_0_.a_ref, bf16[1536,3072]{1,0:T(8,128)(2,1)} %sum_tp_2.1.b_ref), custom_call_target="tpu_custom_call" | custom-call | flops 7864320 | bytes 31457280 | tf_op jit(solution)/shard_map/join/pallas_call | solution.py:354
  (25 shorter events, 0.3 us)
Async XLA Ops:
  6.5 86.8 %all-gather.9.cloned.1.call-start = ((), (), s32[]{:S(2)}) async-start(), calls=%async_computation | async-start | bytes 17694720 | tf_op jit(solution)/shard_map/all_gather | solution.py:381
  10.8 5.4 copy-start.3
  10.9 199.5 %all-gather.11.cloned.1.call-start = ((), (), s32[]{:S(2)}) async-start(), calls=%async_computation.1 | async-start | bytes 11796480 | tf_op jit(solution)/shard_map/all_gather | solution.py:382
  11.7 466.0 %all-gather.13.cloned.1.call-start = ((), (), s32[]{:S(2)}) async-start(), calls=%async_computation.2 | async-start | bytes 41287680 | tf_op jit(solution)/shard_map/all_gather | solution.py:383
  12.5 532.5 %all-gather.15.cloned.1.call-start = ((), (), s32[]{:S(2)}) async-start(), calls=%async_computation.3 | async-start | bytes 41287680 | tf_op jit(solution)/shard_map/all_gather | solution.py:384
  13.1 603.5 %all-gather.17.cloned.1.call-start = ((), (), s32[]{:S(2)}) async-start(), calls=%async_computation.4 | async-start | bytes 16515072 | tf_op jit(solution)/shard_map/all_gather | solution.py:386
  16.1 720.5 %all-gather.19.cloned.1.call-start = ((), (), s32[]{:S(2)}) async-start(), calls=%async_computation.5 | async-start | bytes 24772608 | tf_op jit(solution)/shard_map/all_gather | solution.py:387
  16.3 11.9 %copy-start.2 = (f32[5120]{0:T(1024)S(1)}, f32[5120]{0:T(1024)}, u32[]{:S(2)}) copy-start(f32[5120]{0:T(1024)} %param.15) | copy-start | bytes 61444
  126.5 6.3 copy-start.4
  126.5 6.4 copy-start.5
  128.8 4.1 collective-permute-start
  137.4 2.4 copy-start
  208.7 1.7 copy-start.1
Sparse Core Ops, SparseCore 0:
  11.0 82.2 all-gather.8
  94.9 56.4 all-gather.10
  153.0 168.5 all-gather.12
  323.1 167.3 all-gather.14
  491.9 72.6 all-gather.16
  566.1 104.8 all-gather.18

commit v4 on v3

--- a/solution.py
+++ b/solution.py
@@ -69,19 +69,18 @@
     seg_rows = per_seg * blk
     qi = pl.program_id(1)
     true_seg = table_ref[4 + qi // per_seg]
-    within = lax.rem(qi, per_seg) * blk
     scale = (head_dim ** -0.5) * 1.4426950408889634
     m_sc[...] = jnp.full(m_sc.shape, -1e30, F32)
     l_sc[...] = jnp.zeros(l_sc.shape, F32)
     acc_sc[...] = jnp.zeros(acc_sc.shape, F32)
 
-    def step(j, masked):
-        rows = pl.ds(pl.multiple_of(table_ref[j] * seg_rows, seg_rows), seg_rows)
+    def step(j, n_keys, within):
+        rows = pl.ds(pl.multiple_of(table_ref[j] * seg_rows, seg_rows), n_keys)
         k, vt = k_ref[rows, :], vt_ref[:, rows]
         for h in range(group):
             q = q_ref[:, h * head_dim:(h + 1) * head_dim]
             s = lax.dot_general(k, q, (((1,), (1,)), ((), ())), preferred_element_type=F32) * scale
-            if masked:
+            if within is not None:
                 keep = lax.broadcasted_iota(jnp.int32, s.shape, 0) <= lax.broadcasted_iota(jnp.int32, s.shape, 1) + within
                 s = jnp.where(keep, s, -1e30)
             m_old = m_sc[h]
@@ -93,11 +92,15 @@
             m_sc[h] = m_new
 
     def body(j, carry):
-        step(j, False)
+        step(j, seg_rows, None)
         return carry
 
     lax.fori_loop(0, true_seg, body, 0)
-    step(true_seg, True)
+    for w in range(per_seg):
+        @pl.when(lax.rem(qi, per_seg) == w)
+        def _():
+            step(true_seg, (w + 1) * blk, w * blk)
+
     for h in range(group):
         o_ref[:, h * head_dim:(h + 1) * head_dim] = (acc_sc[h] / l_sc[h]).T.astype(BF16)
 
@@ -236,14 +239,16 @@
             return carry
 
         lax.fori_loop(0, rows // step, one, 0)
-        for i in range(2):
-            hop3(s, i).start()
+        if not with_norm:
+            for i in range(2):
+                hop3(s, i).start()
         local(s).start()
         if with_norm:
             keep(s).start()
 
     def local(s):
-        return pltpu.make_async_copy(norm.at[s], out_hbm.at[rows_of(me, s), :], o_sem.at[s, 0])
+        where = pl.ds(pl.multiple_of(s * rows, rows), rows) if with_norm else rows_of(me, s)
+        return pltpu.make_async_copy(norm.at[s], out_hbm.at[where, :], o_sem.at[s, 0])
 
     def keep(s):
         return pltpu.make_async_copy(own.at[s], own_hbm.at[pl.ds(pl.multiple_of(s * rows, rows), rows), :], o_sem.at[s, 1])
@@ -282,13 +287,14 @@
         def _():
             stage_c(t - 2)
 
-        @pl.when(t >= 3)
-        def _():
-            stage_d(t - 3)
+        if not with_norm:
+            @pl.when(t >= 3)
+            def _():
+                stage_d(t - 3)
 
         return carry
 
-    lax.fori_loop(0, N_SUB + 3, tick, 0)
+    lax.fori_loop(0, N_SUB + (2 if with_norm else 3), tick, 0)
 
     def drain(s, carry):
         local(s).wait()
@@ -297,9 +303,10 @@
         for i in range(2):
             hop1(s, i).wait_send()
             hop2(s, i).wait_send()
-            hop3(s, i).wait_send()
-            hop4(s, i).wait_send()
-            arrive4(s, i).wait_recv()
+            if not with_norm:
+                hop3(s, i).wait_send()
+                hop4(s, i).wait_send()
+                arrive4(s, i).wait_recv()
         return carry
 
     lax.fori_loop(0, N_SUB, drain, 0)
@@ -311,9 +318,7 @@
     cols = n_w * n_cols
     block = tokens // n_tp
     rows = block // N_SUB
-    out_shape = [jax.ShapeDtypeStruct((tokens, cols), BF16)]
-    if with_norm:
-        out_shape = [jax.ShapeDtypeStruct((block, cols), BF16)] + out_shape
+    out_shape = [jax.ShapeDtypeStruct((block, cols), BF16)] * 2 if with_norm else [jax.ShapeDtypeStruct((tokens, cols), BF16)]
     dma = pltpu.SemaphoreType.DMA
     small = (N_SUB, rows, cols) if with_norm else (1, 16, 128)
     scratch = [
@@ -339,6 +344,155 @@
     )(lhs, w, res, gain, *after)
 
 
+def gate_kernel(n_tp, own_hbm, w_hbm, all_hbm, gate_hbm, w, xs, ys, w_sem, x_sem, y_sem, l_sem, s1, r1, s2, r2):
+    block, depth = own_hbm.shape
+    part = block // 2
+    half = depth // 2
+    cols = w.shape[1]
+    n_chunks = w_sem.shape[0]
+    chunk = cols // n_chunks
+    me = lax.axis_index("tp")
+    right, left = lax.rem(me + 1, n_tp), lax.rem(me + n_tp - 1, n_tp)
+    far = lax.rem(me + 2, n_tp)
+    sides = (right, left)
+    halves = (pl.ds(0, half), pl.ds(half, half))
+
+    def rows_of(b, p):
+        return pl.ds(pl.multiple_of(b * block + p * part, part), part)
+
+    def part_of(p):
+        return pl.ds(pl.multiple_of(p * part, part), part)
+
+    def w_copy(n):
+        at = pl.ds(pl.multiple_of(n * chunk, chunk), chunk)
+        return pltpu.make_async_copy(w_hbm.at[:, at], w.at[:, at], w_sem.at[n])
+
+    def remote(src, dst, send, recv, dev):
+        return pltpu.make_async_remote_copy(src_ref=src, dst_ref=dst, send_sem=send, recv_sem=recv, device_id={"tp": dev}, device_id_type=MESH)
+
+    def hop1(p, i):
+        return remote(own_hbm.at[part_of(p), :], all_hbm.at[rows_of(me, p), :], s1.at[p, i], r1.at[p, i], sides[i])
+
+    def hop2(p, i):
+        where = all_hbm.at[rows_of(sides[1 - i], p), halves[i]]
+        return remote(where, where, s2.at[p, i], r2.at[p, i], sides[i])
+
+    def arrive1(p, i):
+        where = all_hbm.at[rows_of(sides[1 - i], p), :]
+        return remote(own_hbm.at[part_of(p), :], where, s1.at[p, i], r1.at[p, i], sides[i])
+
+    def arrive2(p, i):
+        where = all_hbm.at[rows_of(far, p), halves[i]]
+        return remote(where, where, s2.at[p, i], r2.at[p, i], sides[i])
+
+    def y_copy(k, rows):
+        return pltpu.make_async_copy(ys.at[part_of(k)], gate_hbm.at[rows, :], y_sem.at[k])
+
+    barrier = pltpu.get_barrier_semaphore()
+    for dev in sides:
+        pl.semaphore_signal(barrier, inc=1, device_id={"tp": dev}, device_id_type=MESH)
+    pl.semaphore_wait(barrier, 2)
+    for p in range(2):
+        for i in range(2):
+            hop1(p, i).start()
+    own_copies = [pltpu.make_async_copy(own_hbm.at[part_of(p), :], xs.at[part_of(p)], x_sem.at[p]) for p in range(2)]
+    for c in own_copies:
+        c.start()
+    for n in range(n_chunks):
+        w_copy(n).start()
+    for c in own_copies:
+        c.wait()
+    local_copies = [pltpu.make_async_copy(xs.at[part_of(p)], all_hbm.at[rows_of(me, p), :], l_sem.at[p]) for p in range(2)]
+    for c in local_copies:
+        c.start()
+
+    def unit(u, carry):
+        p = jnp.maximum(u - 1, 0)
+        where = [rows_of(jnp.where(u == 0, me, sides[1 - k]), jnp.where(u == 0, k, p)) for k in range(2)]
+
+        @pl.when(u >= 1)
+        def _():
+            for i in range(2):
+                arrive1(p, i).wait_recv()
+                hop2(p, i).start()
+
+            @pl.when(u == 1)
+            def _():
+                for c in local_copies:
+                    c.wait()
+
+            loads = [pltpu.make_async_copy(all_hbm.at[where[k], :], xs.at[part_of(k)], x_sem.at[k]) for k in range(2)]
+            for c in loads:
+                c.start()
+            for k in range(2):
+                y_copy(k, where[k]).wait()
+            for c in loads:
+                c.wait()
+
+        def one(n, c):
+            at = pl.ds(pl.multiple_of(n * chunk, chunk), chunk)
+
+            @pl.when(u == 0)
+            def _():
+                w_copy(n).wait()
+
+            ys[:, at] = jnp.dot(xs[...], w[:, at], preferred_element_type=F32)
+            return c
+
+        lax.fori_loop(0, n_chunks, one, 0)
+        for k in range(2):
+            y_copy(k, where[k]).start()
+        return carry
+
+    lax.fori_loop(0, 3, unit, 0)
+    y_copy(0, rows_of(far, 0)).wait()
+    y_copy(1, rows_of(far, 1)).wait()
+
+    def last(p, carry):
+        for i in range(2):
+            arrive2(p, i).wait_recv()
+        load = pltpu.make_async_copy(all_hbm.at[rows_of(far, p), :], xs.at[part_of(p)], x_sem.at[p])
+        load.start()
+        load.wait()
+
+        def one(n, c):
+            at = pl.ds(pl.multiple_of(n * chunk, chunk), chunk)
+            ys[part_of(p), at] = jnp.dot(xs[part_of(p), :], w[:, at], preferred_element_type=F32)
+            return c
+
+        lax.fori_loop(0, n_chunks, one, 0)
+        y_copy(p, rows_of(far, p)).start()
+        return carry
+
+    lax.fori_loop(0, 2, last, 0)
+    for p in range(2):
+        y_copy(p, rows_of(far, p)).wait()
+        for i in range(2):
+            hop1(p, i).wait_send()
+            hop2(p, i).wait_send()
+
+
+def gather_and_gate(n_tp, own, w, collective_id):
+    block, depth = own.shape
+    cols = w.shape[1]
+    tokens = n_tp * block
+    chunk = next(c for c in (512, 256, 128) if cols % c == 0)
+    dma = pltpu.SemaphoreType.DMA
+    return pl.pallas_call(
+        functools.partial(gate_kernel, n_tp),
+        out_shape=[jax.ShapeDtypeStruct((tokens, depth), BF16), jax.ShapeDtypeStruct((tokens, cols), F32)],
+        in_specs=[ANY, ANY],
+        out_specs=[ANY, ANY],
+        scratch_shapes=[
+            pltpu.VMEM((depth, cols), BF16), pltpu.VMEM((block, depth), BF16), pltpu.VMEM((block, cols), F32),
+            dma((cols // chunk,)), dma((2,)), dma((2,)), dma((2,)),
+        ] + [dma((2, 2))] * 4,
+        compiler_params=pltpu.CompilerParams(collective_id=collective_id, has_side_effects=True, vmem_limit_bytes=VMEM_BIG),
+        cost_estimate=pl.CostEstimate(flops=2 * tokens * cols * depth * 3, bytes_accessed=2 * (tokens * depth + depth * cols + 2 * tokens * cols), transcendentals=0),
+        name="gather_gate",
+    )(own, w)
+
+
 def join_kernel(n_w, a_ref, b_ref, o_ref):
     wa, wb = a_ref.shape[1] // n_w, b_ref.shape[1] // n_w
     for d in range(n_w):
@@ -383,11 +537,11 @@
         full_gate = lax.all_gather(w_gate, GROUP_AXES, axis=0, tiled=True)
         full_up = lax.all_gather(w_up, GROUP_AXES, axis=0, tiled=True)
         cut = (share * 2 // 5) // 128 * 128
-        full_down0 = lax.all_gather(w_down[:, :cut], GROUP_AXES, axis=0, tiled=False)
-        full_down1 = lax.all_gather(w_down[:, cut:], GROUP_AXES, axis=0, tiled=False)
-
         x = hidden[0]
         normed = rms_norm(x.astype(F32), attn_gain)
+        down0, down1, normed = lax.optimization_barrier((w_down[:, :cut], w_down[:, cut:], normed))
+        full_down0 = lax.all_gather(down0, GROUP_AXES, axis=0, tiled=False)
+        full_down1 = lax.all_gather(down1, GROUP_AXES, axis=0, tiled=False)
         cos, sin = rope_tables(positions[0], head_dim)
         qkv = project_qkv(normed, full_qkv, cos, sin, heads + kv_heads)
         kv = qkv[:, heads * head_dim:]
@@ -397,8 +551,8 @@
         kv_all = jnp.concatenate([kv, kv_peer], axis=0)
         k_all, vt_all = kv_all[:, :kv_heads * head_dim], kv_all[:, kv_heads * head_dim:].T
         mixed = attention(qkv, k_all, vt_all, table, heads, kv_heads, head_dim)
-        mid_own, normed_mlp = sum_over_tp(n_tp, mixed, full_out, x, attn_gain_row(mlp_gain), 0, True, 0)
-        gate_proj = jnp.dot(normed_mlp, full_gate, preferred_element_type=F32)
+        mid_own, normed_own = sum_over_tp(n_tp, mixed, full_out, x, attn_gain_row(mlp_gain), 0, True, 0)
+        normed_mlp, gate_proj = gather_and_gate(n_tp, normed_own, full_gate, 3)
         up_proj = jnp.dot(normed_mlp, full_up, preferred_element_type=F32)
         act = (jax.nn.silu(gate_proj) * up_proj).astype(BF16)
         piece0, = sum_over_tp(n_tp, act, full_down0, mid_own, attn_gain_row(mlp_gain), 0, False, 1)

time: 936 us -> 885 us (0.946)
  matrix products: 139 us -> 71.8 us
  Pallas kernels: 681 us -> 694 us
    pallas_call x0 -> x1, Pallas kernels: none -> 142 us  [gather_and_gate(): pl.pallas_call(functools.partial(gate_kernel, n_tp), out_shape=[jax.Shape...]
    pallas_call x3, Pallas kernels: 567 us -> 444 us  [sum_over_tp(): pl.pallas_call(functools.partial(sum_kernel, n_tp, col_off, with_norm, le...]
    dot_general x1 -> x0, matrix products: 67.3 us -> none  [layer_local(): gate_proj = jnp.dot(normed_mlp, full_gate, preferred_element_type=F32)]
  transfers between devices with their start and end apart: 7 -> 7, of which waited for: 1 -> 4; matrix products, arithmetic and copies ran while one was open for 19% -> 13% of each run, Pallas kernels for 52% -> 57%
where the time goes in v4:
time: 885 us
  Pallas kernels  694 us (78%)
  matrix products  71.8 us (8%)
  waiting for transfers between devices  54.8 us (6%)
  other arithmetic  31.8 us (4%)
  local copies, waits for them, and re-layouts  17.4 us (2%)
  between operations  13.7 us (2%)
    pallas_call x3, Pallas kernels, sum_over_tp(): pl.pallas_call(functools.partial(sum_kernel, n_tp, col_off, with_norm, le...  444 us
    pallas_call x1, Pallas kernels, gather_and_gate(): pl.pallas_call(functools.partial(gate_kernel, n_tp), out_shape=[jax.Shape...  142 us
    dot_general x1, matrix products, layer_local(): up_proj = jnp.dot(normed_mlp, full_up, preferred_element_type=F32)  71.8 us
    pallas_call x1, Pallas kernels, attention(): pl.pallas_call(functools.partial(attn_kernel, group, head_dim, per_seg),...  62.9 us
    all_gather x1, waiting for transfers between devices, layer_local(): full_qkv = lax.all_gather(w_qkv, GROUP_AXES, axis=0, tiled=True)  45.7 us
    pallas_call x1, Pallas kernels, project_qkv(): pl.pallas_call(functools.partial(qkv_kernel, head_dim, rope_heads), grid=...  33.2 us
  transfers between devices with their start and end apart: 7, of which 4 were waited for; matrix products, arithmetic and copies ran while one was open for 13% of the time, Pallas kernels for 57%

profile of v4, /device:TPU:97, one launch (start us, length us, event | category | flops | bytes accessed | tf_op | source)
XLA Modules:
  0.0 884.6 jit_solution(3368523332333595762)
XLA Ops:
  6.6 1.7 copy.25
  8.2 1.2 copy_bitcast_fusion.1
  9.4 1.4 pad_maximum_fusion
  10.9 0.7 all-gather.11.cloned.1.call-update
  11.7 0.7 all-gather.13.cloned.1.call-update
  12.5 0.6 all-gather.15.cloned.1.call-update
  13.2 3.6 slice.16
  16.8 2.9 slice.15
  19.7 8.4 fusion
  28.2 14.7 %fusion.2.a_ref = bf16[1536,5120]{1,0:T(8,128)(2,1)} fusion(f32[5120]{0:T(1024)S(1)} %copy-done.2, f32[1536]{0:T(1024)S(1)} %add_rsqrt_fusion, bf16[1,1536,5120]{2,1,0:T(8,128)(2,1)} %param.13), kind=kLoop, calls=%fused_computation.4 | loop fusion | flops 31457280 | bytes 31483904 | tf_op jit(solution)/shard_map/convert_element_type | solution.py:23
  43.0 0.1 all-gather.19.cloned.1.call-start
  43.1 2.8 fusion.5
  45.9 1.7 pad_maximum_fusion.2
  47.6 45.7 %all-gather.9.cloned.1.call-done.w_ref = bf16[5120,1536]{1,0:T(8,128)(2,1)} async-done(((bf16[640,1536]{1,0:T(8,128)(2,1)}), bf16[5120,1536]{1,0:T(8,128)(2,1)}) %all-gather.9.cloned.1.call-update) | async-done | bytes 15728656 | tf_op jit(solution)/shard_map/all_gather | solution.py:535
  93.3 33.2 %qkv.1.q_ref = bf16[1536,1536]{1,0:T(8,128)(2,1)} custom-call(bf16[1536,5120]{1,0:T(8,128)(2,1)} %fusion.2.a_ref, bf16[5120,1536]{1,0:T(8,128)(2,1)} %all-gather.9.cloned.1.call-done.w_ref, f32[1536,128]{1,0:T(8,128)} %get-tuple-element.26.cos_ref, f32[1536,128]{1,0:T(8,128)} %get-tuple-element.27.sin_ref), custom_call_target="tpu_custom_call" | custom-call | flops 24159191040 | bytes 36175872 | tf_op jit(solution)/shard_map/qkv/pallas_call | solution.py:50
  126.5 1.5 slice.20
  128.0 0.7 copy.18
  128.7 0.4 collective-permute-start
  129.2 3.6 collective-permute-done
  132.8 2.8 fusion.4
  135.6 1.7 copy.17.k_ref
  137.4 2.3 copy-done
  139.7 62.9 %attn.1.lhs_hbm = bf16[1536,1024]{1,0:T(8,128)(2,1)S(1)} custom-call(s32[6]{0:T(128)S(1)} %broadcast_select_fusion.table_ref, bf16[1536,1536]{1,0:T(8,128)(2,1)S(1)} %copy-done, bf16[3072,256]{1,0:T(8,128)(2,1)S(1)} %copy.17.k_ref, bf16[256,3072]{1,0:T(8,128)(2,1)S(1)} %get-tuple-element.19.vt_ref), custom_call_target="tpu_custom_call" | custom-call | flops 19327352832 | bytes 9437184 | tf_op jit(solution)/shard_map/attn/pallas_call | solution.py:114
  202.6 1.7 copy-done.1
  204.2 143.7 %sum_tp_0.1 = (bf16[384,5120]{1,0:T(8,128)(2,1)}, bf16[384,5120]{1,0:T(8,128)(2,1)}) custom-call(bf16[1536,1024]{1,0:T(8,128)(2,1)} %copy-done.1, bf16[8,1024,640]{2,1,0:T(8,128)(2,1)} %all-gather.11.cloned.1.call-done.w_hbm, bf16[1536,5120]{1,0:T(8,128)(2,1)} %bitcast.22, f32[1,5120]{1,0:T(1,128)} %bitcast.30), custom_call_target="tpu_custom_call" | custom-call | flops 471859200000 | bytes 45088768 | tf_op jit(solution)/shard_map/sum_tp_0/pallas_call | solution.py:335
  347.9 141.6 %gather_gate.1 = (bf16[1536,5120]{1,0:T(8,128)(2,1)}, f32[1536,3584]{1,0:T(8,128)}) custom-call(bf16[384,5120]{1,0:T(8,128)(2,1)} %get-tuple-element.13.own_hbm, bf16[5120,3584]{1,0:T(8,128)(2,1)} %all-gather.13.cloned.1.call-done.w_hbm), custom_call_target="tpu_custom_call" | custom-call | flops 169114337280 | bytes 74448896 | tf_op jit(solution)/shard_map/gather_gate/pallas_call | solution.py:481
  489.5 0.9 all-gather.15.cloned.1.call-done
  490.5 71.8 %multiply_convert_fusion.lhs_hbm = bf16[1536,3584]{1,0:T(8,128)(2,1)} fusion(f32[1536,3584]{1,0:T(8,128)} %get-tuple-element.14, bf16[1536,5120]{1,0:T(8,128)(2,1)} %get-tuple-element.15, bf16[5120,3584]{1,0:T(8,128)(2,1)} %all-gather.15.cloned.1.call-done), kind=kOutput, calls=%fused_computation.5 | convolution fusion | flops 56404475904 | bytes 85458944 | tf_op jit(solution)/shard_map/dot_general | solution.py:556
  562.3 2.3 all-gather.17.cloned.1.call-done
  564.6 122.7 %sum_tp_1.1.refs_0_.a_ref = bf16[1536,2048]{1,0:T(8,128)(2,1)} custom-call(bf16[1536,3584]{1,0:T(8,128)(2,1)} %multiply_convert_fusion.lhs_hbm, bf16[8,3584,256]{2,1,0:T(8,128)(2,1)} %bitcast.29, bf16[384,5120]{1,0:T(8,128)(2,1)} %get-tuple-element.17.res_hbm, f32[1,5120]{1,0:T(1,128)} %bitcast.31), custom_call_target="tpu_custom_call" | custom-call | flops 188743680000 | bytes 38273024 | tf_op jit(solution)/shard_map/sum_tp_1/pallas_call | solution.py:335
  687.3 178.1 %sum_tp_2.1.b_ref = bf16[1536,3072]{1,0:T(8,128)(2,1)} custom-call(bf16[1536,3584]{1,0:T(8,128)(2,1)} %multiply_convert_fusion.lhs_hbm, bf16[8,3584,384]{2,1,0:T(8,128)(2,1)} %bitcast.28, bf16[384,5120]{1,0:T(8,128)(2,1)} %get-tuple-element.17.res_hbm, f32[1,5120]{1,0:T(1,128)} %bitcast.32, bf16[1536,2048]{1,0:T(8,128)(2,1)} %sum_tp_1.1.refs_0_.a_ref), custom_call_target="tpu_custom_call" | custom-call | flops 283115520000 | bytes 51904512 | tf_op jit(solution)/shard_map/sum_tp_2/pallas_call | solution.py:335
  865.4 12.3 %join.1 = bf16[1536,5120]{1,0:T(8,128)(2,1)} custom-call(bf16[1536,2048]{1,0:T(8,128)(2,1)} %sum_tp_1.1.refs_0_.a_ref, bf16[1536,3072]{1,0:T(8,128)(2,1)} %sum_tp_2.1.b_ref), custom_call_target="tpu_custom_call" | custom-call | flops 7864320 | bytes 31457280 | tf_op jit(solution)/shard_map/join/pallas_call | solution.py:508
  (25 shorter events, 0.5 us)
Async XLA Ops:
  6.5 86.7 %all-gather.9.cloned.1.call-start = ((), (), s32[]{:S(2)}) async-start(), calls=%async_computation | async-start | bytes 17694720 | tf_op jit(solution)/shard_map/all_gather | solution.py:535
  10.9 193.4 %all-gather.11.cloned.1.call-start = ((), (), s32[]{:S(2)}) async-start(), calls=%async_computation.1 | async-start | bytes 11796480 | tf_op jit(solution)/shard_map/all_gather | solution.py:536
  11.7 336.3 %all-gather.13.cloned.1.call-start = ((), (), s32[]{:S(2)}) async-start(), calls=%async_computation.2 | async-start | bytes 41287680 | tf_op jit(solution)/shard_map/all_gather | solution.py:537
  12.5 478.0 %all-gather.15.cloned.1.call-start = ((), (), s32[]{:S(2)}) async-start(), calls=%async_computation.3 | async-start | bytes 41287680 | tf_op jit(solution)/shard_map/all_gather | solution.py:538
  13.1 551.5 %all-gather.17.cloned.1.call-start = ((), (), s32[]{:S(2)}) async-start(), calls=%async_computation.4 | async-start | bytes 16515072 | tf_op jit(solution)/shard_map/all_gather | solution.py:543
  19.7 8.5 copy-start.2
  28.2 14.9 %copy-start.3 = (s32[1,1536]{1,0:T(1,128)S(1)}, s32[1,1536]{1,0:T(1,128)}, u32[]{:S(2)}) copy-start(s32[1,1536]{1,0:T(1,128)} %param.14) | copy-start | bytes 18436
  43.0 644.3 %all-gather.19.cloned.1.call-start = ((), (), s32[]{:S(2)}) async-start(), calls=%async_computation.5 | async-start | bytes 24772608 | tf_op jit(solution)/shard_map/all_gather | solution.py:544
  126.5 2.7 copy-start.4
  126.5 2.7 copy-start.5
  128.7 4.1 collective-permute-start
  137.3 2.4 copy-start
  202.6 1.7 copy-start.1
Sparse Core Ops, SparseCore 0:
  11.0 82.2 all-gather.8
  94.9 56.4 all-gather.10
  153.0 168.5 all-gather.12
  323.0 167.3 all-gather.14
  491.9 72.6 all-gather.16
  566.0 104.8 all-gather.18

commit v5 on v4

--- a/solution.py
+++ b/solution.py
@@ -10,7 +10,7 @@
 ROPE_THETA = 500000.0
 NORM_EPS = 1e-5
 GROUP_AXES = ('fsdp', 'cp')
-N_SUB = 6
+N_SUB = 8
 F32 = jnp.float32
 BF16 = jnp.bfloat16
 MESH = pl.DeviceIdType.MESH
@@ -155,11 +155,24 @@
     def w_copy(d):
         return pltpu.make_async_copy(w_hbm.at[d], w.at[d], w_sem.at[d])
 
-    lhs_copies = [pltpu.make_async_copy(lhs_hbm.at[pl.ds(b * block, block), :], lhs.at[b], l_sem.at[b]) for b in range(n_tp)]
-    for c in lhs_copies:
-        c.start()
+    def rows_of(b, s):
+        return pl.ds(pl.multiple_of(b * block + s * rows, rows), rows)
+
+    def lhs_copy(s, b):
+        at = pl.ds(pl.multiple_of(s * rows, rows), rows)
+        return pltpu.make_async_copy(lhs_hbm.at[rows_of(b, s), :], lhs.at[b, at, :], l_sem.at[s, b])
+
+    for b in range(n_tp):
+        lhs_copy(0, b).start()
     for d in range(n_w):
         w_copy(d).start()
+
+    def load(s, carry):
+        for b in range(n_tp):
+            lhs_copy(s, b).start()
+        return carry
+
+    lax.fori_loop(1, N_SUB, load, 0)
     my_rows = pl.ds(pl.multiple_of(me * block, block), block)
     if with_norm:
         res_copies = [pltpu.make_async_copy(res_hbm.at[my_rows, :], res, r_sem.at[0])]
@@ -177,9 +190,6 @@
     def remote(src, dst, send, recv, dev):
         return pltpu.make_async_remote_copy(src_ref=src, dst_ref=dst, send_sem=send, recv_sem=recv, device_id={"tp": dev}, device_id_type=MESH)
 
-    def rows_of(b, s):
-        return pl.ds(pl.multiple_of(b * block + s * rows, rows), rows)
-
     def hop1(s, i):
         return remote(part.at[s, far, :, halves[i]], in1.at[s, i], s1.at[s, i], r1.at[s, i], sides[i])
 
@@ -196,6 +206,8 @@
 
     def stage_a(s):
         at = pl.ds(pl.multiple_of(s * rows, rows), rows)
+        for b in range(n_tp):
+            lhs_copy(s, b).wait()
 
         def one(d, carry):
             @pl.when(s == 0)
@@ -205,11 +217,13 @@
             left_rows = lhs[:, at, :].reshape(n_tp * rows, depth)
             prod = jnp.dot(left_rows, w[d], preferred_element_type=F32).astype(BF16)
             part[s, :, :, pl.ds(pl.multiple_of(d * n_cols, n_cols), n_cols)] = prod.reshape(n_tp, rows, n_cols)
+            for i in range(2):
+                @pl.when(d == (i + 1) * (n_w // 2) - 1)
+                def _():
+                    hop1(s, i).start()
             return carry
 
         lax.fori_loop(0, n_w, one, 0)
-        for i in range(2):
-            hop1(s, i).start()
 
     def stage_b(s):
         for i in range(2):
@@ -265,9 +279,6 @@
         for i in range(2):
             arrive3(s, i).wait_recv()
             hop4(s, i).start()
-
-    for c in lhs_copies:
-        c.wait()
 
     def tick(t, carry):
         @pl.when(t < N_SUB)
@@ -330,7 +341,7 @@
         pltpu.VMEM((block, cols), BF16),
         pltpu.VMEM(small, BF16),
         pltpu.VMEM((N_SUB, rows, cols), BF16),
-        dma((n_w,)), dma((n_tp,)), dma((n_w,)), dma((N_SUB, 2)),
+        dma((n_w,)), dma((N_SUB, n_tp)), dma((n_w,)), dma((N_SUB, 2)),
     ] + [dma((N_SUB, 2))] * 8
     return pl.pallas_call(
         functools.partial(sum_kernel, n_tp, col_off, with_norm, len(after)),
@@ -503,7 +514,7 @@
 
 def join_columns(a, b, n_w):
     tokens = a.shape[0]
-    rows = min(256, tokens)
+    rows = min(128, tokens)
     cols = a.shape[1] + b.shape[1]
     return pl.pallas_call(
         functools.partial(join_kernel, n_w),

time: 885 us -> 877 us (level)
  Pallas kernels: 694 us -> 682 us
    pallas_call x3, Pallas kernels: 444 us -> 430 us  [sum_over_tp(): pl.pallas_call(functools.partial(sum_kernel, n_tp, col_off, with_norm, le...]
  transfers between devices with their start and end apart: 7 -> 7, of which waited for: 4 -> 4; matrix products, arithmetic and copies ran while one was open for 13% -> 13% of each run, Pallas kernels for 57% -> 56%
where the time goes in v5:
time: 877 us; the launch traced here: 876 us
  Pallas kernels  682 us (78%)
  matrix products  71.8 us (8%)
  waiting for transfers between devices  58.5 us (7%)
  other arithmetic  31.8 us (4%)
  local copies, waits for them, and re-layouts  17.4 us (2%)
  between operations  13.7 us (2%)
    pallas_call x3, Pallas kernels, sum_over_tp(): pl.pallas_call(functools.partial(sum_kernel, n_tp, col_off, with_norm, le...  430 us
    pallas_call x1, Pallas kernels, gather_and_gate(): pl.pallas_call(functools.partial(gate_kernel, n_tp), out_shape=[jax.Shape...  141 us
    dot_general x1, matrix products, layer_local(): up_proj = jnp.dot(normed_mlp, full_up, preferred_element_type=F32)  71.8 us
    pallas_call x1, Pallas kernels, attention(): pl.pallas_call(functools.partial(attn_kernel, group, head_dim, per_seg),...  62.9 us
    all_gather x1, waiting for transfers between devices, layer_local(): full_qkv = lax.all_gather(w_qkv, GROUP_AXES, axis=0, tiled=True)  45.7 us
    pallas_call x1, Pallas kernels, project_qkv(): pl.pallas_call(functools.partial(qkv_kernel, head_dim, rope_heads), grid=...  33.2 us
  transfers between devices with their start and end apart: 7, of which 4 were waited for; matrix products, arithmetic and copies ran while one was open for 13% of the time, Pallas kernels for 56%

profile of v5, /device:TPU:97, one launch (start us, length us, event | category | flops | bytes accessed | tf_op | source)
XLA Modules:
  0.0 876.0 jit_solution(4147066818641047006)
XLA Ops:
  6.6 1.7 copy.25
  8.2 1.2 copy_bitcast_fusion.1
  9.4 1.4 pad_maximum_fusion
  10.9 0.7 all-gather.11.cloned.1.call-update
  11.7 0.7 all-gather.13.cloned.1.call-update
  12.5 0.6 all-gather.15.cloned.1.call-update
  13.2 3.6 slice.16
  16.8 2.9 slice.15
  19.7 8.4 fusion
  28.2 14.7 %fusion.2.a_ref = bf16[1536,5120]{1,0:T(8,128)(2,1)} fusion(f32[5120]{0:T(1024)S(1)} %copy-done.2, f32[1536]{0:T(1024)S(1)} %add_rsqrt_fusion, bf16[1,1536,5120]{2,1,0:T(8,128)(2,1)} %param.13), kind=kLoop, calls=%fused_computation.4 | loop fusion | flops 31457280 | bytes 31483904 | tf_op jit(solution)/shard_map/convert_element_type | solution.py:23
  43.0 0.1 all-gather.19.cloned.1.call-start
  43.1 2.8 fusion.5
  45.9 1.7 pad_maximum_fusion.2
  47.6 45.7 %all-gather.9.cloned.1.call-done.w_ref = bf16[5120,1536]{1,0:T(8,128)(2,1)} async-done(((bf16[640,1536]{1,0:T(8,128)(2,1)}), bf16[5120,1536]{1,0:T(8,128)(2,1)}) %all-gather.9.cloned.1.call-update) | async-done | bytes 15728656 | tf_op jit(solution)/shard_map/all_gather | solution.py:546
  93.3 33.2 %qkv.1.q_ref = bf16[1536,1536]{1,0:T(8,128)(2,1)} custom-call(bf16[1536,5120]{1,0:T(8,128)(2,1)} %fusion.2.a_ref, bf16[5120,1536]{1,0:T(8,128)(2,1)} %all-gather.9.cloned.1.call-done.w_ref, f32[1536,128]{1,0:T(8,128)} %get-tuple-element.26.cos_ref, f32[1536,128]{1,0:T(8,128)} %get-tuple-element.27.sin_ref), custom_call_target="tpu_custom_call" | custom-call | flops 24159191040 | bytes 36175872 | tf_op jit(solution)/shard_map/qkv/pallas_call | solution.py:50
  126.5 1.5 slice.20
  128.0 0.7 copy.18
  128.7 0.4 collective-permute-start
  129.2 3.6 collective-permute-done
  132.8 2.8 fusion.4
  135.6 1.7 copy.17.k_ref
  137.4 2.3 copy-done
  139.7 62.9 %attn.1.lhs_hbm = bf16[1536,1024]{1,0:T(8,128)(2,1)S(1)} custom-call(s32[6]{0:T(128)S(1)} %broadcast_select_fusion.table_ref, bf16[1536,1536]{1,0:T(8,128)(2,1)S(1)} %copy-done, bf16[3072,256]{1,0:T(8,128)(2,1)S(1)} %copy.17.k_ref, bf16[256,3072]{1,0:T(8,128)(2,1)S(1)} %get-tuple-element.19.vt_ref), custom_call_target="tpu_custom_call" | custom-call | flops 19327352832 | bytes 9437184 | tf_op jit(solution)/shard_map/attn/pallas_call | solution.py:114
  202.6 1.7 copy-done.1
  204.2 140.3 %sum_tp_0.1 = (bf16[384,5120]{1,0:T(8,128)(2,1)}, bf16[384,5120]{1,0:T(8,128)(2,1)}) custom-call(bf16[1536,1024]{1,0:T(8,128)(2,1)} %copy-done.1, bf16[8,1024,640]{2,1,0:T(8,128)(2,1)} %all-gather.11.cloned.1.call-done.w_hbm, bf16[1536,5120]{1,0:T(8,128)(2,1)} %bitcast.22, f32[1,5120]{1,0:T(1,128)} %bitcast.30), custom_call_target="tpu_custom_call" | custom-call | flops 471859200000 | bytes 45088768 | tf_op jit(solution)/shard_map/sum_tp_0/pallas_call | solution.py:346
  344.6 141.2 %gather_gate.1 = (bf16[1536,5120]{1,0:T(8,128)(2,1)}, f32[1536,3584]{1,0:T(8,128)}) custom-call(bf16[384,5120]{1,0:T(8,128)(2,1)} %get-tuple-element.13.own_hbm, bf16[5120,3584]{1,0:T(8,128)(2,1)} %all-gather.13.cloned.1.call-done.w_hbm), custom_call_target="tpu_custom_call" | custom-call | flops 169114337280 | bytes 74448896 | tf_op jit(solution)/shard_map/gather_gate/pallas_call | solution.py:492
  485.8 4.6 all-gather.15.cloned.1.call-done
  490.5 71.8 %multiply_convert_fusion.lhs_hbm = bf16[1536,3584]{1,0:T(8,128)(2,1)} fusion(f32[1536,3584]{1,0:T(8,128)} %get-tuple-element.14, bf16[1536,5120]{1,0:T(8,128)(2,1)} %get-tuple-element.15, bf16[5120,3584]{1,0:T(8,128)(2,1)} %all-gather.15.cloned.1.call-done), kind=kOutput, calls=%fused_computation.5 | convolution fusion | flops 56404475904 | bytes 85458944 | tf_op jit(solution)/shard_map/dot_general | solution.py:567
  562.3 2.3 all-gather.17.cloned.1.call-done
  564.6 116.9 %sum_tp_1.1.refs_0_.a_ref = bf16[1536,2048]{1,0:T(8,128)(2,1)} custom-call(bf16[1536,3584]{1,0:T(8,128)(2,1)} %multiply_convert_fusion.lhs_hbm, bf16[8,3584,256]{2,1,0:T(8,128)(2,1)} %bitcast.29, bf16[384,5120]{1,0:T(8,128)(2,1)} %get-tuple-element.17.res_hbm, f32[1,5120]{1,0:T(1,128)} %bitcast.31), custom_call_target="tpu_custom_call" | custom-call | flops 188743680000 | bytes 38273024 | tf_op jit(solution)/shard_map/sum_tp_1/pallas_call | solution.py:346
  681.5 172.6 %sum_tp_2.1.b_ref = bf16[1536,3072]{1,0:T(8,128)(2,1)} custom-call(bf16[1536,3584]{1,0:T(8,128)(2,1)} %multiply_convert_fusion.lhs_hbm, bf16[8,3584,384]{2,1,0:T(8,128)(2,1)} %bitcast.28, bf16[384,5120]{1,0:T(8,128)(2,1)} %get-tuple-element.17.res_hbm, f32[1,5120]{1,0:T(1,128)} %bitcast.32, bf16[1536,2048]{1,0:T(8,128)(2,1)} %sum_tp_1.1.refs_0_.a_ref), custom_call_target="tpu_custom_call" | custom-call | flops 283115520000 | bytes 51904512 | tf_op jit(solution)/shard_map/sum_tp_2/pallas_call | solution.py:346
  854.1 15.0 %join.1 = bf16[1536,5120]{1,0:T(8,128)(2,1)} custom-call(bf16[1536,2048]{1,0:T(8,128)(2,1)} %sum_tp_1.1.refs_0_.a_ref, bf16[1536,3072]{1,0:T(8,128)(2,1)} %sum_tp_2.1.b_ref), custom_call_target="tpu_custom_call" | custom-call | flops 7864320 | bytes 31457280 | tf_op jit(solution)/shard_map/join/pallas_call | solution.py:519
  (25 shorter events, 0.5 us)
Async XLA Ops:
  6.5 86.7 %all-gather.9.cloned.1.call-start = ((), (), s32[]{:S(2)}) async-start(), calls=%async_computation | async-start | bytes 17694720 | tf_op jit(solution)/shard_map/all_gather | solution.py:546
  10.9 193.4 %all-gather.11.cloned.1.call-start = ((), (), s32[]{:S(2)}) async-start(), calls=%async_computation.1 | async-start | bytes 11796480 | tf_op jit(solution)/shard_map/all_gather | solution.py:547
  11.7 332.9 %all-gather.13.cloned.1.call-start = ((), (), s32[]{:S(2)}) async-start(), calls=%async_computation.2 | async-start | bytes 41287680 | tf_op jit(solution)/shard_map/all_gather | solution.py:548
  12.5 478.0 %all-gather.15.cloned.1.call-start = ((), (), s32[]{:S(2)}) async-start(), calls=%async_computation.3 | async-start | bytes 41287680 | tf_op jit(solution)/shard_map/all_gather | solution.py:549
  13.1 551.5 %all-gather.17.cloned.1.call-start = ((), (), s32[]{:S(2)}) async-start(), calls=%async_computation.4 | async-start | bytes 16515072 | tf_op jit(solution)/shard_map/all_gather | solution.py:554
  19.7 8.5 copy-start.2
  28.2 14.9 %copy-start.3 = (s32[1,1536]{1,0:T(1,128)S(1)}, s32[1,1536]{1,0:T(1,128)}, u32[]{:S(2)}) copy-start(s32[1,1536]{1,0:T(1,128)} %param.14) | copy-start | bytes 18436
  43.0 638.5 %all-gather.19.cloned.1.call-start = ((), (), s32[]{:S(2)}) async-start(), calls=%async_computation.5 | async-start | bytes 24772608 | tf_op jit(solution)/shard_map/all_gather | solution.py:555
  126.5 2.7 copy-start.4
  126.5 2.7 copy-start.5
  128.7 4.1 collective-permute-start
  137.3 2.4 copy-start
  202.6 1.7 copy-start.1
Sparse Core Ops, SparseCore 0:
  11.0 82.2 all-gather.8
  94.9 56.4 all-gather.10
  153.0 168.5 all-gather.12
  323.0 167.3 all-gather.14
  491.9 72.6 all-gather.16
  566.0 104.9 all-gather.18

commit v6 on v5

--- a/solution.py
+++ b/solution.py
@@ -10,7 +10,7 @@
 ROPE_THETA = 500000.0
 NORM_EPS = 1e-5
 GROUP_AXES = ('fsdp', 'cp')
-N_SUB = 8
+N_SUB = 12
 F32 = jnp.float32
 BF16 = jnp.bfloat16
 MESH = pl.DeviceIdType.MESH
@@ -514,7 +514,7 @@
 
 def join_columns(a, b, n_w):
     tokens = a.shape[0]
-    rows = min(128, tokens)
+    rows = min(384, tokens)
     cols = a.shape[1] + b.shape[1]
     return pl.pallas_call(
         functools.partial(join_kernel, n_w),
@@ -522,6 +522,7 @@
         out_shape=jax.ShapeDtypeStruct((tokens, cols), BF16),
         in_specs=[pl.BlockSpec((rows, a.shape[1]), lambda i: (i, 0)), pl.BlockSpec((rows, b.shape[1]), lambda i: (i, 0))],
         out_specs=pl.BlockSpec((rows, cols), lambda i: (i, 0)),
+        compiler_params=pltpu.CompilerParams(vmem_limit_bytes=VMEM_BIG),
         cost_estimate=pl.CostEstimate(flops=tokens * cols, bytes_accessed=4 * tokens * cols, transcendentals=0),
         name="join",
     )(a, b)

time: 877 us -> 872 us (level)
  transfers between devices with their start and end apart: 7 -> 7, of which waited for: 4 -> 4; matrix products, arithmetic and copies ran while one was open for 13% -> 13% of each run, Pallas kernels for 56% -> 57%
where the time goes in v6:
time: 872 us; the launch traced here: 871 us
  Pallas kernels  677 us (78%)
  matrix products  71.8 us (8%)
  waiting for transfers between devices  58.8 us (7%)
  other arithmetic  31.8 us (4%)
  local copies, waits for them, and re-layouts  17.4 us (2%)
  between operations  13.7 us (2%)
    pallas_call x3, Pallas kernels, sum_over_tp(): pl.pallas_call(functools.partial(sum_kernel, n_tp, col_off, with_norm, le...  429 us
    pallas_call x1, Pallas kernels, gather_and_gate(): pl.pallas_call(functools.partial(gate_kernel, n_tp), out_shape=[jax.Shape...  141 us
    dot_general x1, matrix products, layer_local(): up_proj = jnp.dot(normed_mlp, full_up, preferred_element_type=F32)  71.8 us
    pallas_call x1, Pallas kernels, attention(): pl.pallas_call(functools.partial(attn_kernel, group, head_dim, per_seg),...  62.9 us
    all_gather x1, waiting for transfers between devices, layer_local(): full_qkv = lax.all_gather(w_qkv, GROUP_AXES, axis=0, tiled=True)  45.7 us
    pallas_call x1, Pallas kernels, project_qkv(): pl.pallas_call(functools.partial(qkv_kernel, head_dim, rope_heads), grid=...  33.2 us
  transfers between devices with their start and end apart: 7, of which 4 were waited for; matrix products, arithmetic and copies ran while one was open for 13% of the time, Pallas kernels for 57%

profile of v6, /device:TPU:97, one launch (start us, length us, event | category | flops | bytes accessed | tf_op | source)
XLA Modules:
  0.0 871.4 jit_solution(16748283644107622057)
XLA Ops:
  6.6 1.7 copy.25
  8.2 1.2 copy_bitcast_fusion.1
  9.4 1.4 pad_maximum_fusion
  10.9 0.7 all-gather.11.cloned.1.call-update
  11.7 0.7 all-gather.13.cloned.1.call-update
  12.5 0.6 all-gather.15.cloned.1.call-update
  13.2 3.6 slice.16
  16.8 2.9 slice.15
  19.7 8.4 fusion
  28.2 14.7 %fusion.2.a_ref = bf16[1536,5120]{1,0:T(8,128)(2,1)} fusion(f32[5120]{0:T(1024)S(1)} %copy-done.2, f32[1536]{0:T(1024)S(1)} %add_rsqrt_fusion, bf16[1,1536,5120]{2,1,0:T(8,128)(2,1)} %param.13), kind=kLoop, calls=%fused_computation.4 | loop fusion | flops 31457280 | bytes 31483904 | tf_op jit(solution)/shard_map/convert_element_type | solution.py:23
  43.0 0.1 all-gather.19.cloned.1.call-start
  43.1 2.8 fusion.5
  45.9 1.7 pad_maximum_fusion.2
  47.6 45.7 %all-gather.9.cloned.1.call-done.w_ref = bf16[5120,1536]{1,0:T(8,128)(2,1)} async-done(((bf16[640,1536]{1,0:T(8,128)(2,1)}), bf16[5120,1536]{1,0:T(8,128)(2,1)}) %all-gather.9.cloned.1.call-update) | async-done | bytes 15728656 | tf_op jit(solution)/shard_map/all_gather | solution.py:547
  93.3 33.2 %qkv.1.q_ref = bf16[1536,1536]{1,0:T(8,128)(2,1)} custom-call(bf16[1536,5120]{1,0:T(8,128)(2,1)} %fusion.2.a_ref, bf16[5120,1536]{1,0:T(8,128)(2,1)} %all-gather.9.cloned.1.call-done.w_ref, f32[1536,128]{1,0:T(8,128)} %get-tuple-element.26.cos_ref, f32[1536,128]{1,0:T(8,128)} %get-tuple-element.27.sin_ref), custom_call_target="tpu_custom_call" | custom-call | flops 24159191040 | bytes 36175872 | tf_op jit(solution)/shard_map/qkv/pallas_call | solution.py:50
  126.5 1.5 slice.20
  128.0 0.7 copy.18
  128.7 0.4 collective-permute-start
  129.2 3.6 collective-permute-done
  132.8 2.8 fusion.4
  135.6 1.7 copy.17.k_ref
  137.4 2.3 copy-done
  139.7 62.9 %attn.1.lhs_hbm = bf16[1536,1024]{1,0:T(8,128)(2,1)S(1)} custom-call(s32[6]{0:T(128)S(1)} %broadcast_select_fusion.table_ref, bf16[1536,1536]{1,0:T(8,128)(2,1)S(1)} %copy-done, bf16[3072,256]{1,0:T(8,128)(2,1)S(1)} %copy.17.k_ref, bf16[256,3072]{1,0:T(8,128)(2,1)S(1)} %get-tuple-element.19.vt_ref), custom_call_target="tpu_custom_call" | custom-call | flops 19327352832 | bytes 9437184 | tf_op jit(solution)/shard_map/attn/pallas_call | solution.py:114
  202.6 1.7 copy-done.1
  204.2 139.9 %sum_tp_0.1 = (bf16[384,5120]{1,0:T(8,128)(2,1)}, bf16[384,5120]{1,0:T(8,128)(2,1)}) custom-call(bf16[1536,1024]{1,0:T(8,128)(2,1)} %copy-done.1, bf16[8,1024,640]{2,1,0:T(8,128)(2,1)} %all-gather.11.cloned.1.call-done.w_hbm, bf16[1536,5120]{1,0:T(8,128)(2,1)} %bitcast.22, f32[1,5120]{1,0:T(1,128)} %bitcast.30), custom_call_target="tpu_custom_call" | custom-call | flops 471859200000 | bytes 45088768 | tf_op jit(solution)/shard_map/sum_tp_0/pallas_call | solution.py:346
  344.2 141.3 %gather_gate.1 = (bf16[1536,5120]{1,0:T(8,128)(2,1)}, f32[1536,3584]{1,0:T(8,128)}) custom-call(bf16[384,5120]{1,0:T(8,128)(2,1)} %get-tuple-element.13.own_hbm, bf16[5120,3584]{1,0:T(8,128)(2,1)} %all-gather.13.cloned.1.call-done.w_hbm), custom_call_target="tpu_custom_call" | custom-call | flops 169114337280 | bytes 74448896 | tf_op jit(solution)/shard_map/gather_gate/pallas_call | solution.py:492
  485.5 5.0 all-gather.15.cloned.1.call-done
  490.5 71.8 %multiply_convert_fusion.lhs_hbm = bf16[1536,3584]{1,0:T(8,128)(2,1)} fusion(f32[1536,3584]{1,0:T(8,128)} %get-tuple-element.14, bf16[1536,5120]{1,0:T(8,128)(2,1)} %get-tuple-element.15, bf16[5120,3584]{1,0:T(8,128)(2,1)} %all-gather.15.cloned.1.call-done), kind=kOutput, calls=%fused_computation.5 | convolution fusion | flops 56404475904 | bytes 85458944 | tf_op jit(solution)/shard_map/dot_general | solution.py:568
  562.3 2.3 all-gather.17.cloned.1.call-done
  564.6 117.5 %sum_tp_1.1.refs_0_.a_ref = bf16[1536,2048]{1,0:T(8,128)(2,1)} custom-call(bf16[1536,3584]{1,0:T(8,128)(2,1)} %multiply_convert_fusion.lhs_hbm, bf16[8,3584,256]{2,1,0:T(8,128)(2,1)} %bitcast.29, bf16[384,5120]{1,0:T(8,128)(2,1)} %get-tuple-element.17.res_hbm, f32[1,5120]{1,0:T(1,128)} %bitcast.31), custom_call_target="tpu_custom_call" | custom-call | flops 188743680000 | bytes 38273024 | tf_op jit(solution)/shard_map/sum_tp_1/pallas_call | solution.py:346
  682.1 171.2 %sum_tp_2.1.b_ref = bf16[1536,3072]{1,0:T(8,128)(2,1)} custom-call(bf16[1536,3584]{1,0:T(8,128)(2,1)} %multiply_convert_fusion.lhs_hbm, bf16[8,3584,384]{2,1,0:T(8,128)(2,1)} %bitcast.28, bf16[384,5120]{1,0:T(8,128)(2,1)} %get-tuple-element.17.res_hbm, f32[1,5120]{1,0:T(1,128)} %bitcast.32, bf16[1536,2048]{1,0:T(8,128)(2,1)} %sum_tp_1.1.refs_0_.a_ref), custom_call_target="tpu_custom_call" | custom-call | flops 283115520000 | bytes 51904512 | tf_op jit(solution)/shard_map/sum_tp_2/pallas_call | solution.py:346
  853.3 11.2 %join.1 = bf16[1536,5120]{1,0:T(8,128)(2,1)} custom-call(bf16[1536,2048]{1,0:T(8,128)(2,1)} %sum_tp_1.1.refs_0_.a_ref, bf16[1536,3072]{1,0:T(8,128)(2,1)} %sum_tp_2.1.b_ref), custom_call_target="tpu_custom_call" | custom-call | flops 7864320 | bytes 31457280 | tf_op jit(solution)/shard_map/join/pallas_call | solution.py:519
  (25 shorter events, 0.5 us)
Async XLA Ops:
  6.5 86.7 %all-gather.9.cloned.1.call-start = ((), (), s32[]{:S(2)}) async-start(), calls=%async_computation | async-start | bytes 17694720 | tf_op jit(solution)/shard_map/all_gather | solution.py:547
  10.9 193.4 %all-gather.11.cloned.1.call-start = ((), (), s32[]{:S(2)}) async-start(), calls=%async_computation.1 | async-start | bytes 11796480 | tf_op jit(solution)/shard_map/all_gather | solution.py:548
  11.7 332.5 %all-gather.13.cloned.1.call-start = ((), (), s32[]{:S(2)}) async-start(), calls=%async_computation.2 | async-start | bytes 41287680 | tf_op jit(solution)/shard_map/all_gather | solution.py:549
  12.5 478.0 %all-gather.15.cloned.1.call-start = ((), (), s32[]{:S(2)}) async-start(), calls=%async_computation.3 | async-start | bytes 41287680 | tf_op jit(solution)/shard_map/all_gather | solution.py:550
  13.1 551.5 %all-gather.17.cloned.1.call-start = ((), (), s32[]{:S(2)}) async-start(), calls=%async_computation.4 | async-start | bytes 16515072 | tf_op jit(solution)/shard_map/all_gather | solution.py:555
  19.7 8.5 copy-start.2
  28.2 14.9 %copy-start.3 = (s32[1,1536]{1,0:T(1,128)S(1)}, s32[1,1536]{1,0:T(1,128)}, u32[]{:S(2)}) copy-start(s32[1,1536]{1,0:T(1,128)} %param.14) | copy-start | bytes 18436
  43.0 639.1 %all-gather.19.cloned.1.call-start = ((), (), s32[]{:S(2)}) async-start(), calls=%async_computation.5 | async-start | bytes 24772608 | tf_op jit(solution)/shard_map/all_gather | solution.py:556
  126.5 2.7 copy-start.4
  126.5 2.7 copy-start.5
  128.7 4.1 collective-permute-start
  137.3 2.4 copy-start
  202.6 1.7 copy-start.1
Sparse Core Ops, SparseCore 0:
  11.0 82.2 all-gather.8
  94.9 56.4 all-gather.10
  153.0 168.5 all-gather.12
  323.0 167.3 all-gather.14
  491.9 72.6 all-gather.16
  566.0 104.8 all-gather.18
